TPU v7x, 8 devices: a whole 2x2x1 slice. The times are simulated.
8 devices in a mesh: data: 1 (over z), col: 2 (over y), row: 4 (over x, core).
Axes of the slice: x: 2, y: 2, z: 1, core: 2. Of those that a mesh axis runs over, the one named last changes fastest.
Arguments:
- tokens: bfloat16 [4096, 2048], P(('data', 'row'), 'col')
- w_qkv: bfloat16 [2048, 2560], P('row', 'col')
- w_out: bfloat16 [2048, 2048], P('row', 'col')
- doc_ids: int32 [4096], P(('data', 'row'))
Outputs:
- output: bfloat16 [4096, 2048], P(('data', 'row'), 'col')
All inputs are finite; a program needn't handle non-finite values.
Results may differ from a plain program's by a relative error of at most 0.00401571.
Values are sent between devices in bfloat16 or wider.
A program may use at most 1 GiB of HBM per device.

v0:
```python
import jax
import jax.numpy as jnp
from jax import lax
from jax.sharding import PartitionSpec as P

HEAD_DIM = 128


def block_size(row_count, score_width):
    q_blk = row_count
    while q_blk % 16 == 0 and q_blk * score_width > 4194304:
        q_blk = q_blk // 2
    return q_blk


def solution(mesh):
    score_scale = HEAD_DIM ** -0.5

    def local_block(tokens, w_qkv, w_out, doc_ids):
        rows_loc, cols_loc = tokens.shape
        heads_loc = cols_loc // HEAD_DIM
        groups_loc = (w_qkv.shape[1] - cols_loc) // (2 * HEAD_DIM)
        group_ratio = heads_loc // groups_loc
        x_panel = lax.all_gather(tokens, "col", axis=1, tiled=True)
        w_panel = lax.all_gather(w_qkv, "row", axis=0, tiled=True)
        qkv_rows = jnp.dot(x_panel, w_panel, preferred_element_type=jnp.float32).astype(jnp.bfloat16)
        qkv_rows = qkv_rows.reshape(rows_loc, groups_loc, group_ratio + 2, HEAD_DIM)
        kv_all = lax.all_gather(qkv_rows[:, :, group_ratio:, :], "row", axis=0, tiled=True)
        seg_all = lax.all_gather(doc_ids, "row", axis=0, tiled=True)
        seq_len = kv_all.shape[0]
        key_rows = kv_all[:, :, 0, :]
        value_rows = kv_all[:, :, 1, :]
        q_blk = block_size(rows_loc, heads_loc * seq_len)
        n_steps = rows_loc // q_blk
        q_steps = qkv_rows[:, :, :group_ratio, :].reshape(n_steps, q_blk, groups_loc, group_ratio, HEAD_DIM)

        def attend(block_in):
            q_part, seg_part = block_in
            scores = jnp.einsum("qgrd,kgd->qgrk", q_part, key_rows, preferred_element_type=jnp.float32) * score_scale
            same_doc = seg_part[:, None, None, None] == seg_all[None, None, None, :]
            scores = jnp.where(same_doc, scores, -jnp.inf)
            weights = jax.nn.softmax(scores, axis=-1).astype(jnp.bfloat16)
            context = jnp.einsum("qgrk,kgd->qgrd", weights, value_rows, preferred_element_type=jnp.float32)
            return context.astype(jnp.bfloat16)

        context = lax.map(attend, (q_steps, doc_ids.reshape(n_steps, q_blk)))
        context = context.reshape(rows_loc, cols_loc)
        o_panel = lax.all_gather(context, "col", axis=1, tiled=True)
        wo_panel = lax.all_gather(w_out, "row", axis=0, tiled=True)
        return jnp.dot(o_panel, wo_panel, preferred_element_type=jnp.float32).astype(jnp.bfloat16)

    row_spec = P(("data", "row"), "col")
    weight_spec = P("row", "col")
    return jax.shard_map(local_block, mesh=mesh, in_specs=(row_spec, weight_spec, weight_spec, P(("data", "row"))), out_specs=row_spec, check_vma=False)
```

profile of v0, /device:TPU:0, one launch (start us, length us, event | category | flops | bytes accessed | tf_op | source)
XLA Modules:
  0.0 336.1 jit_solution(6537364255008636492)
XLA Ops:
  6.5 0.7 all-gather.6.cloned.1.call-update
  7.3 0.0 all-gather.8.cloned.1.call-start
  7.3 0.7 all-gather.8.cloned.1.call-update
  8.0 0.0 all-gather.10.cloned.1.call-start
  8.1 57.8 %all-gather.6.cloned.1.call-done = bf16[1024,2048]{1,0:T(8,128)(2,1)} async-done(((bf16[1024,1024]{1,0:T(8,128)(2,1)}), bf16[1024,2048]{1,0:T(8,128)(2,1)}) %all-gather.6.cloned.1.call-update) | async-done | bytes 4194320 | tf_op jit(solution)/shard_map/all_gather | solution.py:24
  65.9 39.1 %all-gather.8.cloned.1.call-done = bf16[2048,1280]{1,0:T(8,128)(2,1)} async-done(((bf16[512,1280]{1,0:T(8,128)(2,1)}), bf16[2048,1280]{1,0:T(8,128)(2,1)}) %all-gather.8.cloned.1.call-update) | async-done | bytes 5242896 | tf_op jit(solution)/shard_map/all_gather | solution.py:25
  105.0 9.9 %convolution_convert_fusion = bf16[1024,1280]{1,0:T(8,128)(2,1)} fusion(bf16[1024,2048]{1,0:T(8,128)(2,1)} %all-gather.6.cloned.1.call-done, bf16[2048,1280]{1,0:T(8,128)(2,1)} %all-gather.8.cloned.1.call-done), kind=kOutput, calls=%fused_computation.20 | convolution fusion | flops 5370019840 | bytes 12058624 | tf_op jit(solution)/shard_map/dot_general | solution.py:26
  114.9 3.0 copy.12
  118.0 0.9 slice.17
  118.8 0.0 all-gather.14.cloned.1.call-start
  118.9 0.5 all-gather.14.cloned.1.call-update
  119.4 0.0 all-gather.12.cloned.1.call-start
  119.5 7.4 %all_gather.18 = s32[4096]{0:T(1024)S(1)} all-gather(s32[1024]{0:T(1024)S(1)} %copy-done.1), channel_id=1, replica_groups=mesh['data'=1,'col'=2,'row'=4] {'row'}, dimensions={0}, use_global_device_ids=true | all-gather | bytes 20480 | tf_op jit(solution)/shard_map/all_gather | solution.py:29
  126.9 1.6 slice.16
  128.5 3.4 %copy.13 = bf16[1024,1,8,128]{3,2,0,1:T(8,128)(2,1)S(1)} copy(bf16[1024,1,8,128]{0,3,2,1:T(8,128)(2,1)} %slice.16) | data formatting | bytes 4194304 | tf_op jit(solution)/shard_map/slice | solution.py:35
  131.9 6.8 %all-gather.10.cloned.1.call-done = bf16[4096,1,2,128]{0,3,2,1:T(8,128)(2,1)} async-done(((bf16[1024,1,2,128]{0,3,2,1:T(8,128)(2,1)}), bf16[4096,1,2,128]{0,3,2,1:T(8,128)(2,1)}) %all-gather.10.cloned.1.call-update) | async-done | bytes 2097168 | tf_op jit(solution)/shard_map/all_gather | solution.py:28
  138.7 3.1 slice_bitcast_fusion
  141.8 1.6 copy.15
  143.4 2.3 copy.16
  145.6 116.5 %while.10 = (s32[]{:T(128)}, bf16[8,128,1,8,128]{4,3,1,0,2:T(8,128)(2,1)}, s32[8,128]{1,0:T(8,128)S(1)}, s32[4096]{0:T(1024)S(1)}, bf16[8,128,1,8,128]{4,3,1,0,2...) while((s32[]{:T(128)}, ...), condition=%wide.region_3.4_spmd, body=%wide.region_0.3_spmd.sunk | while | flops 2198468608 | bytes 60332152 | solution.py:46
  145.7 0.4 broadcast_compare_fusion.2
  146.0 3.1 fusion.29
  149.1 4.8 %fusion.30 = f32[128,8]{0,1:T(8,128)S(1)} fusion(f32[128,8,4096]{2,0,1:T(8,128)S(1)} %get-tuple-element.120, f32[128,8]{0,1:T(8,128)S(1)} %get-tuple-element.121, pred[128,4096]{1,0:T(8,128)(4,1)S(1)} %broadcast_compare_fusion.2), kind=kLoop, calls=%fused_computation.3.clone.1 | loop fusion | flops 16776192 | bytes 17309696 | tf_op jit(solution)/shard_map/while/body/eval_jaxpr/reduce_sum | solution.py:42
  154.0 5.3 %fusion.31 = bf16[1,128,1,8,128]{4,1,3,2,0:T(8,128)(2,1)S(1)} fusion(f32[128,8]{0,1:T(8,128)S(1)} %fusion.30, f32[128,8]{0,1:T(8,128)S(1)} %get-tuple-element.121, f32[128,8,4096]{2,0,1:T(8,128)S(1)} %get-tuple-element.120, pred[128,4096]{1,0:T(8,128)(4,1)S(1)} %broadcast_compare_fusion.2, bf16[4096,1,128]{2,0,1:T(8,128)(2,1)S(1)} %copy-done), kind=kOutput, calls=%fused_computation.8.clone.1 | convolution fusion | flops 1094844416 | bytes 18620416 | tf_op jit(solution)/shard_map/while/body/eval_jaxpr/qgrk,kgd->qgrd/dot_general | solution.py:43
  159.3 0.9 copy_dynamic-update-slice_fusion.2
  160.2 0.4 broadcast_compare_fusion.2
  160.6 3.1 fusion.29
  163.7 4.8 %fusion.30 = f32[128,8]{0,1:T(8,128)S(1)} fusion(f32[128,8,4096]{2,0,1:T(8,128)S(1)} %get-tuple-element.120, f32[128,8]{0,1:T(8,128)S(1)} %get-tuple-element.121, pred[128,4096]{1,0:T(8,128)(4,1)S(1)} %broadcast_compare_fusion.2), kind=kLoop, calls=%fused_computation.3.clone.1 | loop fusion | flops 16776192 | bytes 17309696 | tf_op jit(solution)/shard_map/while/body/eval_jaxpr/reduce_sum | solution.py:42
  168.6 5.3 %fusion.31 = bf16[1,128,1,8,128]{4,1,3,2,0:T(8,128)(2,1)S(1)} fusion(f32[128,8]{0,1:T(8,128)S(1)} %fusion.30, f32[128,8]{0,1:T(8,128)S(1)} %get-tuple-element.121, f32[128,8,4096]{2,0,1:T(8,128)S(1)} %get-tuple-element.120, pred[128,4096]{1,0:T(8,128)(4,1)S(1)} %broadcast_compare_fusion.2, bf16[4096,1,128]{2,0,1:T(8,128)(2,1)S(1)} %copy-done), kind=kOutput, calls=%fused_computation.8.clone.1 | convolution fusion | flops 1094844416 | bytes 18620416 | tf_op jit(solution)/shard_map/while/body/eval_jaxpr/qgrk,kgd->qgrd/dot_general | solution.py:43
  173.9 0.9 copy_dynamic-update-slice_fusion.2
  174.8 0.4 broadcast_compare_fusion.2
  175.2 3.1 fusion.29
  178.3 4.8 %fusion.30 = f32[128,8]{0,1:T(8,128)S(1)} fusion(f32[128,8,4096]{2,0,1:T(8,128)S(1)} %get-tuple-element.120, f32[128,8]{0,1:T(8,128)S(1)} %get-tuple-element.121, pred[128,4096]{1,0:T(8,128)(4,1)S(1)} %broadcast_compare_fusion.2), kind=kLoop, calls=%fused_computation.3.clone.1 | loop fusion | flops 16776192 | bytes 17309696 | tf_op jit(solution)/shard_map/while/body/eval_jaxpr/reduce_sum | solution.py:42
  183.1 5.3 %fusion.31 = bf16[1,128,1,8,128]{4,1,3,2,0:T(8,128)(2,1)S(1)} fusion(f32[128,8]{0,1:T(8,128)S(1)} %fusion.30, f32[128,8]{0,1:T(8,128)S(1)} %get-tuple-element.121, f32[128,8,4096]{2,0,1:T(8,128)S(1)} %get-tuple-element.120, pred[128,4096]{1,0:T(8,128)(4,1)S(1)} %broadcast_compare_fusion.2, bf16[4096,1,128]{2,0,1:T(8,128)(2,1)S(1)} %copy-done), kind=kOutput, calls=%fused_computation.8.clone.1 | convolution fusion | flops 1094844416 | bytes 18620416 | tf_op jit(solution)/shard_map/while/body/eval_jaxpr/qgrk,kgd->qgrd/dot_general | solution.py:43
  188.5 0.9 copy_dynamic-update-slice_fusion.2
  189.4 0.4 broadcast_compare_fusion.2
  189.8 3.1 fusion.29
  192.8 4.8 %fusion.30 = f32[128,8]{0,1:T(8,128)S(1)} fusion(f32[128,8,4096]{2,0,1:T(8,128)S(1)} %get-tuple-element.120, f32[128,8]{0,1:T(8,128)S(1)} %get-tuple-element.121, pred[128,4096]{1,0:T(8,128)(4,1)S(1)} %broadcast_compare_fusion.2), kind=kLoop, calls=%fused_computation.3.clone.1 | loop fusion | flops 16776192 | bytes 17309696 | tf_op jit(solution)/shard_map/while/body/eval_jaxpr/reduce_sum | solution.py:42
  197.7 5.3 %fusion.31 = bf16[1,128,1,8,128]{4,1,3,2,0:T(8,128)(2,1)S(1)} fusion(f32[128,8]{0,1:T(8,128)S(1)} %fusion.30, f32[128,8]{0,1:T(8,128)S(1)} %get-tuple-element.121, f32[128,8,4096]{2,0,1:T(8,128)S(1)} %get-tuple-element.120, pred[128,4096]{1,0:T(8,128)(4,1)S(1)} %broadcast_compare_fusion.2, bf16[4096,1,128]{2,0,1:T(8,128)(2,1)S(1)} %copy-done), kind=kOutput, calls=%fused_computation.8.clone.1 | convolution fusion | flops 1094844416 | bytes 18620416 | tf_op jit(solution)/shard_map/while/body/eval_jaxpr/qgrk,kgd->qgrd/dot_general | solution.py:43
  203.0 0.9 copy_dynamic-update-slice_fusion.2
  203.9 0.4 broadcast_compare_fusion.2
  204.3 3.1 fusion.29
  207.4 4.8 %fusion.30 = f32[128,8]{0,1:T(8,128)S(1)} fusion(f32[128,8,4096]{2,0,1:T(8,128)S(1)} %get-tuple-element.120, f32[128,8]{0,1:T(8,128)S(1)} %get-tuple-element.121, pred[128,4096]{1,0:T(8,128)(4,1)S(1)} %broadcast_compare_fusion.2), kind=kLoop, calls=%fused_computation.3.clone.1 | loop fusion | flops 16776192 | bytes 17309696 | tf_op jit(solution)/shard_map/while/body/eval_jaxpr/reduce_sum | solution.py:42
  212.3 5.3 %fusion.31 = bf16[1,128,1,8,128]{4,1,3,2,0:T(8,128)(2,1)S(1)} fusion(f32[128,8]{0,1:T(8,128)S(1)} %fusion.30, f32[128,8]{0,1:T(8,128)S(1)} %get-tuple-element.121, f32[128,8,4096]{2,0,1:T(8,128)S(1)} %get-tuple-element.120, pred[128,4096]{1,0:T(8,128)(4,1)S(1)} %broadcast_compare_fusion.2, bf16[4096,1,128]{2,0,1:T(8,128)(2,1)S(1)} %copy-done), kind=kOutput, calls=%fused_computation.8.clone.1 | convolution fusion | flops 1094844416 | bytes 18620416 | tf_op jit(solution)/shard_map/while/body/eval_jaxpr/qgrk,kgd->qgrd/dot_general | solution.py:43
  217.6 0.9 copy_dynamic-update-slice_fusion.2
  218.5 0.4 broadcast_compare_fusion.2
  218.9 3.1 fusion.29
  222.0 4.8 %fusion.30 = f32[128,8]{0,1:T(8,128)S(1)} fusion(f32[128,8,4096]{2,0,1:T(8,128)S(1)} %get-tuple-element.120, f32[128,8]{0,1:T(8,128)S(1)} %get-tuple-element.121, pred[128,4096]{1,0:T(8,128)(4,1)S(1)} %broadcast_compare_fusion.2), kind=kLoop, calls=%fused_computation.3.clone.1 | loop fusion | flops 16776192 | bytes 17309696 | tf_op jit(solution)/shard_map/while/body/eval_jaxpr/reduce_sum | solution.py:42
  226.8 5.3 %fusion.31 = bf16[1,128,1,8,128]{4,1,3,2,0:T(8,128)(2,1)S(1)} fusion(f32[128,8]{0,1:T(8,128)S(1)} %fusion.30, f32[128,8]{0,1:T(8,128)S(1)} %get-tuple-element.121, f32[128,8,4096]{2,0,1:T(8,128)S(1)} %get-tuple-element.120, pred[128,4096]{1,0:T(8,128)(4,1)S(1)} %broadcast_compare_fusion.2, bf16[4096,1,128]{2,0,1:T(8,128)(2,1)S(1)} %copy-done), kind=kOutput, calls=%fused_computation.8.clone.1 | convolution fusion | flops 1094844416 | bytes 18620416 | tf_op jit(solution)/shard_map/while/body/eval_jaxpr/qgrk,kgd->qgrd/dot_general | solution.py:43
  232.2 0.9 copy_dynamic-update-slice_fusion.2
  233.1 0.4 broadcast_compare_fusion.2
  233.5 3.1 fusion.29
  236.5 4.8 %fusion.30 = f32[128,8]{0,1:T(8,128)S(1)} fusion(f32[128,8,4096]{2,0,1:T(8,128)S(1)} %get-tuple-element.120, f32[128,8]{0,1:T(8,128)S(1)} %get-tuple-element.121, pred[128,4096]{1,0:T(8,128)(4,1)S(1)} %broadcast_compare_fusion.2), kind=kLoop, calls=%fused_computation.3.clone.1 | loop fusion | flops 16776192 | bytes 17309696 | tf_op jit(solution)/shard_map/while/body/eval_jaxpr/reduce_sum | solution.py:42
  241.4 5.3 %fusion.31 = bf16[1,128,1,8,128]{4,1,3,2,0:T(8,128)(2,1)S(1)} fusion(f32[128,8]{0,1:T(8,128)S(1)} %fusion.30, f32[128,8]{0,1:T(8,128)S(1)} %get-tuple-element.121, f32[128,8,4096]{2,0,1:T(8,128)S(1)} %get-tuple-element.120, pred[128,4096]{1,0:T(8,128)(4,1)S(1)} %broadcast_compare_fusion.2, bf16[4096,1,128]{2,0,1:T(8,128)(2,1)S(1)} %copy-done), kind=kOutput, calls=%fused_computation.8.clone.1 | convolution fusion | flops 1094844416 | bytes 18620416 | tf_op jit(solution)/shard_map/while/body/eval_jaxpr/qgrk,kgd->qgrd/dot_general | solution.py:43
  246.7 0.9 copy_dynamic-update-slice_fusion.2
  247.6 0.4 broadcast_compare_fusion.2
  248.0 3.1 fusion.29
  251.1 4.8 %fusion.30 = f32[128,8]{0,1:T(8,128)S(1)} fusion(f32[128,8,4096]{2,0,1:T(8,128)S(1)} %get-tuple-element.120, f32[128,8]{0,1:T(8,128)S(1)} %get-tuple-element.121, pred[128,4096]{1,0:T(8,128)(4,1)S(1)} %broadcast_compare_fusion.2), kind=kLoop, calls=%fused_computation.3.clone.1 | loop fusion | flops 16776192 | bytes 17309696 | tf_op jit(solution)/shard_map/while/body/eval_jaxpr/reduce_sum | solution.py:42
  256.0 5.3 %fusion.31 = bf16[1,128,1,8,128]{4,1,3,2,0:T(8,128)(2,1)S(1)} fusion(f32[128,8]{0,1:T(8,128)S(1)} %fusion.30, f32[128,8]{0,1:T(8,128)S(1)} %get-tuple-element.121, f32[128,8,4096]{2,0,1:T(8,128)S(1)} %get-tuple-element.120, pred[128,4096]{1,0:T(8,128)(4,1)S(1)} %broadcast_compare_fusion.2, bf16[4096,1,128]{2,0,1:T(8,128)(2,1)S(1)} %copy-done), kind=kOutput, calls=%fused_computation.8.clone.1 | convolution fusion | flops 1094844416 | bytes 18620416 | tf_op jit(solution)/shard_map/while/body/eval_jaxpr/qgrk,kgd->qgrd/dot_general | solution.py:43
  261.3 0.9 copy_dynamic-update-slice_fusion.2
  262.2 3.6 %copy.28 = bf16[128,8,8,128]{3,1,2,0:T(8,128)(2,1)} copy(bf16[128,8,8,128]{3,2,1,0:T(8,128)(2,1)} %bitcast.26) | data formatting | bytes 4194304
  265.8 0.0 all-gather.14.cloned.1.call-done
  265.8 54.4 %all-gather.12.cloned.1.call-done = bf16[1024,2048]{1,0:T(8,128)(2,1)} async-done(((bf16[1024,1024]{1,0:T(8,128)(2,1)}), bf16[1024,2048]{1,0:T(8,128)(2,1)}) %all-gather.12.cloned.1.call-update) | async-done | bytes 4194320 | tf_op jit(solution)/shard_map/all_gather | solution.py:48
  320.3 9.3 %convolution_convert_fusion.1 = bf16[1024,1024]{1,0:T(8,128)(2,1)} fusion(bf16[1024,2048]{1,0:T(8,128)(2,1)} %all-gather.12.cloned.1.call-done, bf16[2048,1024]{1,0:T(8,128)(2,1)} %all-gather.14.cloned.1.call-done), kind=kOutput, calls=%fused_computation.22 | convolution fusion | flops 4296015872 | bytes 10485760 | tf_op jit(solution)/shard_map/dot_general | solution.py:50
  (38 shorter events, 0.3 us)
Async XLA Ops:
  6.5 59.4 %all-gather.6.cloned.1.call-start = ((), (), s32[]{:S(2)}) async-start(), calls=%async_computation | async-start | bytes 6291456 | tf_op jit(solution)/shard_map/all_gather | solution.py:24
  7.3 97.7 %all-gather.8.cloned.1.call-start = ((), (), s32[]{:S(2)}) async-start(), calls=%async_computation.1 | async-start | bytes 6553600 | tf_op jit(solution)/shard_map/all_gather | solution.py:25
  8.0 130.6 %all-gather.10.cloned.1.call-start = ((), (), s32[]{:S(2)}) async-start(), calls=%async_computation.2 | async-start | bytes 2621440 | tf_op jit(solution)/shard_map/all_gather | solution.py:28
  114.9 4.5 %copy-start.1 = (s32[1024]{0:T(1024)S(1)}, s32[1024]{0:T(1024)}, u32[]{:S(2)}) copy-start(s32[1024]{0:T(1024)} %param.9) | copy-start | bytes 12292
  118.8 147.0 %all-gather.14.cloned.1.call-start = ((), (), s32[]{:S(2)}) async-start(), calls=%async_computation.4 | async-start | bytes 5242880 | tf_op jit(solution)/shard_map/all_gather | solution.py:49
  119.4 200.8 %all-gather.12.cloned.1.call-start = ((), (), s32[]{:S(2)}) async-start(), calls=%async_computation.3 | async-start | bytes 6291456 | tf_op jit(solution)/shard_map/all_gather | solution.py:48
  149.1 4.9 %copy-start = (bf16[4096,1,128]{2,0,1:T(8,128)(2,1)S(1)}, bf16[4096,1,128]{2,0,1:T(8,128)(2,1)}, u32[]{:S(2)}) copy-start(bf16[4096,1,128]{2,0,1:T(8,128)(2,1)} %get-tuple-element.144) | copy-start | bytes 3145732 | tf_op jit(solution)/shard_map/while
  163.7 4.9 %copy-start = (bf16[4096,1,128]{2,0,1:T(8,128)(2,1)S(1)}, bf16[4096,1,128]{2,0,1:T(8,128)(2,1)}, u32[]{:S(2)}) copy-start(bf16[4096,1,128]{2,0,1:T(8,128)(2,1)} %get-tuple-element.144) | copy-start | bytes 3145732 | tf_op jit(solution)/shard_map/while
  178.3 4.9 %copy-start = (bf16[4096,1,128]{2,0,1:T(8,128)(2,1)S(1)}, bf16[4096,1,128]{2,0,1:T(8,128)(2,1)}, u32[]{:S(2)}) copy-start(bf16[4096,1,128]{2,0,1:T(8,128)(2,1)} %get-tuple-element.144) | copy-start | bytes 3145732 | tf_op jit(solution)/shard_map/while
  192.8 4.9 %copy-start = (bf16[4096,1,128]{2,0,1:T(8,128)(2,1)S(1)}, bf16[4096,1,128]{2,0,1:T(8,128)(2,1)}, u32[]{:S(2)}) copy-start(bf16[4096,1,128]{2,0,1:T(8,128)(2,1)} %get-tuple-element.144) | copy-start | bytes 3145732 | tf_op jit(solution)/shard_map/while
  207.4 4.9 %copy-start = (bf16[4096,1,128]{2,0,1:T(8,128)(2,1)S(1)}, bf16[4096,1,128]{2,0,1:T(8,128)(2,1)}, u32[]{:S(2)}) copy-start(bf16[4096,1,128]{2,0,1:T(8,128)(2,1)} %get-tuple-element.144) | copy-start | bytes 3145732 | tf_op jit(solution)/shard_map/while
  222.0 4.9 %copy-start = (bf16[4096,1,128]{2,0,1:T(8,128)(2,1)S(1)}, bf16[4096,1,128]{2,0,1:T(8,128)(2,1)}, u32[]{:S(2)}) copy-start(bf16[4096,1,128]{2,0,1:T(8,128)(2,1)} %get-tuple-element.144) | copy-start | bytes 3145732 | tf_op jit(solution)/shard_map/while
  236.5 4.9 %copy-start = (bf16[4096,1,128]{2,0,1:T(8,128)(2,1)S(1)}, bf16[4096,1,128]{2,0,1:T(8,128)(2,1)}, u32[]{:S(2)}) copy-start(bf16[4096,1,128]{2,0,1:T(8,128)(2,1)} %get-tuple-element.144) | copy-start | bytes 3145732 | tf_op jit(solution)/shard_map/while
  251.1 4.9 %copy-start = (bf16[4096,1,128]{2,0,1:T(8,128)(2,1)S(1)}, bf16[4096,1,128]{2,0,1:T(8,128)(2,1)}, u32[]{:S(2)}) copy-start(bf16[4096,1,128]{2,0,1:T(8,128)(2,1)} %get-tuple-element.144) | copy-start | bytes 3145732 | tf_op jit(solution)/shard_map/while
Sparse Core Ops, SparseCore 0:
  8.8 57.0 all-gather.5
  67.4 37.5 all-gather.7
  119.0 19.6 all-gather.9
  140.0 31.6 all-gather.13
  265.9 54.2 all-gather.11
where the time goes:
time: 336 us
  waiting for transfers between devices  160 us (48%)
  matrix products  86.4 us (26%)
  other arithmetic  41.6 us (12%)
  local copies, waits for them, and re-layouts  26.8 us (8%)
  between operations  13.2 us (4%)
  blocking collectives  7.39 us (2%)
    all_gather x1, waiting for transfers between devices, local_block(): x_panel = lax.all_gather(tokens, 'col', axis=1, tiled=True)  57.8 us
    all_gather x1, waiting for transfers between devices, local_block(): o_panel = lax.all_gather(context, 'col', axis=1, tiled=True)  54.4 us
    dot_general x8, matrix products, attend(): jnp.einsum('qgrk,kgd->qgrd', weights, value_rows, preferred_element_type=...  42.6 us
    all_gather x1, waiting for transfers between devices, local_block(): w_panel = lax.all_gather(w_qkv, 'row', axis=0, tiled=True)  39.1 us
    reduce_sum x8, other arithmetic, attend(): weights = jax.nn.softmax(scores, axis=-1).astype(jnp.bfloat16)  38.8 us
    dot_general x8, matrix products, attend(): jnp.einsum('qgrd,kgd->qgrk', q_part, key_rows, preferred_element_type=jnp...  24.6 us
    dot_general x1, matrix products, local_block(): jnp.dot(x_panel, w_panel, preferred_element_type=jnp.float32)  9.95 us
    dot_general x1, matrix products, local_block(): jnp.dot(o_panel, wo_panel, preferred_element_type=jnp.float32)  9.27 us
  transfers between devices with their start and end apart: 5, of which 4 were waited for; matrix products, arithmetic and copies ran while one was open for 39% of the time, Pallas kernels for 0%

commit v1 on v0

v1 whole, which is shorter than its diff:
```python
import functools
import math

import jax
import jax.numpy as jnp
from jax import lax
from jax.experimental import pallas as pl
from jax.experimental.pallas import tpu as pltpu
from jax.sharding import PartitionSpec as P

HEAD_DIM = 128
MESH = pl.DeviceIdType.MESH

ROWS = 1024
HID = 1024
SEQ = 4096
HEADS = 8
QKV = 1280
SHARD = 512
QB = 256
KC = 512
CHUNK = 256
N_CHUNK = ROWS // CHUNK
W_PIECES = 4
W_ROWS = SHARD // W_PIECES
TILES = HEADS * (ROWS // QB)
CORE, XP, DIAG = 0, 1, 2
EXP_SCALE = math.log2(math.e) / math.sqrt(HEAD_DIM)
NT = (((1,), (1,)), ((), ()))


def kernel(
    tok_hbm, w_hbm, wo_hbm, doc_hbm, out_hbm,
    tok_own, tok_peer, w_buf, wo_buf, doc_buf, kcol, bias, q_buf, k_buf, vt_buf, s0, s1, ctx_own, ctx_peer, out_buf,
    loc_sem, tok_send, tok_recv, wx_send, wx_recv, wc_send, wc_recv, wf_send, wf_recv,
    ox_send, ox_recv, oc_send, oc_recv, of_send, of_recv, doc_send, doc_recv, kv_send, kv_recv, ctx_send, ctx_recv, out_sem,
):
    d, y, r = lax.axis_index("data"), lax.axis_index("col"), lax.axis_index("row")
    x, core = r // 2, r % 2
    row_of = {CORE: x * 2 + (1 - core), XP: (1 - x) * 2 + core, DIAG: (1 - x) * 2 + (1 - core)}
    y_peer = (d, 1 - y, r)
    peer = {k: (d, y, v) for k, v in row_of.items()}

    barrier = pltpu.get_barrier_semaphore()
    for p in (y_peer, peer[CORE], peer[XP], peer[DIAG]):
        pl.semaphore_signal(barrier, inc=1, device_id=p, device_id_type=MESH)
    pl.semaphore_wait(barrier, 4)

    def rcopy(src, dst, ssem, rsem, dev):
        return pltpu.make_async_remote_copy(
            src_ref=src, dst_ref=dst, send_sem=ssem, recv_sem=rsem, device_id=dev, device_id_type=MESH
        )

    def shard_rows(row, piece=0, size=SHARD):
        return pl.ds(pl.multiple_of(row * SHARD + piece * size, size), size)

    tok_copies = []
    for c in range(N_CHUNK):
        rows = pl.ds(c * CHUNK, CHUNK)
        cp = rcopy(tok_hbm.at[rows], tok_peer.at[rows], tok_send.at[c], tok_recv.at[c], y_peer)
        cp.start()
        tok_copies.append(cp)
    doc_copies = []
    for k in (CORE, XP, DIAG):
        cp = rcopy(doc_hbm, doc_buf.at[r], doc_send.at[k], doc_recv.at[k], peer[k])
        cp.start()
        doc_copies.append(cp)
    wx_copies = []
    for p in range(W_PIECES):
        cp = rcopy(
            w_hbm.at[pl.ds(p * W_ROWS, W_ROWS)], w_buf.at[shard_rows(r, p, W_ROWS)], wx_send.at[p], wx_recv.at[p], peer[XP]
        )
        cp.start()
        wx_copies.append(cp)
    wc_copy = rcopy(w_hbm, w_buf.at[shard_rows(r)], wc_send, wc_recv, peer[CORE])
    wc_copy.start()
    oc_copy = rcopy(wo_hbm, wo_buf.at[shard_rows(r)], oc_send, oc_recv, peer[CORE])
    oc_copy.start()
    doc_local = pltpu.make_async_copy(doc_hbm, doc_buf.at[r], loc_sem.at[0])
    doc_local.start()
    w_local = pltpu.make_async_copy(w_hbm, w_buf.at[shard_rows(r)], loc_sem.at[1])
    w_local.start()
    tok_local = pltpu.make_async_copy(tok_hbm, tok_own, loc_sem.at[2])
    tok_local.start()
    wo_local = pltpu.make_async_copy(wo_hbm, wo_buf.at[shard_rows(r)], loc_sem.at[3])
    wo_local.start()

    doc_local.wait()
    for cp in doc_copies:
        cp.wait_recv()

    def spread(i, carry):
        line = doc_buf[i // 8, pl.ds(i % 8, 1), :]
        kcol[pl.ds(pl.multiple_of(i * 128, 128), 128), :] = jnp.transpose(jnp.broadcast_to(line, (128, 128)))
        return carry

    lax.fori_loop(0, SEQ // 128, spread, 0)

    def mask_tile(i, carry):
        lanes = pl.ds(pl.multiple_of((i // 16) * 128, 128), 128)
        keys = pl.ds(pl.multiple_of((i % 16) * 256, 256), 256)
        line = doc_buf[r, pl.ds(i // 16, 1), :]
        bias[keys, lanes] = jnp.where(kcol[keys, :] == line, 0.0, -jnp.inf)
        return carry

    lax.fori_loop(0, 8 * 16, mask_tile, 0)

    wf_copies = []
    for p in range(W_PIECES):
        wx_copies[p].wait_recv()
        rows = shard_rows(row_of[XP], p, W_ROWS)
        cp = rcopy(w_buf.at[rows], w_buf.at[rows], wf_send.at[p], wf_recv.at[p], peer[CORE])
        cp.start()
        wf_copies.append(cp)
    w_local.wait()
    tok_local.wait()
    wc_copy.wait_recv()
    for cp in wf_copies:
        cp.wait_recv()

    own_half = pl.ds(pl.multiple_of(y * HID, HID), HID)
    peer_half = pl.ds(pl.multiple_of((1 - y) * HID, HID), HID)

    def project(rows, cols):
        return jnp.dot(tok_own[rows, :], w_buf[own_half, cols], preferred_element_type=jnp.float32) + jnp.dot(
            tok_peer[rows, :], w_buf[peer_half, cols], preferred_element_type=jnp.float32
        )

    kv_copies = []
    for c in range(N_CHUNK):
        rows = pl.ds(c * CHUNK, CHUNK)
        tok_copies[c].wait_recv()
        kv = project(rows, pl.ds(HID, 2 * HEAD_DIM)).astype(jnp.bfloat16)
        krows = pl.ds(pl.multiple_of(r * ROWS + c * CHUNK, CHUNK), CHUNK)
        k_buf[krows, :] = kv[:, :HEAD_DIM]
        vt_buf[:, krows] = jnp.transpose(kv[:, HEAD_DIM:])
        for k in (DIAG, XP, CORE):
            cp = rcopy(k_buf.at[krows], k_buf.at[krows], kv_send.at[c, k, 0], kv_recv.at[c, k, 0], peer[k])
            cp.start()
            kv_copies.append(cp)
            cp = rcopy(vt_buf.at[:, krows], vt_buf.at[:, krows], kv_send.at[c, k, 1], kv_recv.at[c, k, 1], peer[k])
            cp.start()
            kv_copies.append(cp)

        def q_tile(n, carry):
            cols = pl.ds(pl.multiple_of(n * 256, 256), 256)
            q_buf[rows, cols] = project(rows, cols).astype(jnp.bfloat16)
            return carry

        lax.fori_loop(0, HID // 256, q_tile, 0)

    for cp in kv_copies:
        cp.wait_recv()

    ox_copy = rcopy(wo_hbm, wo_buf.at[shard_rows(r)], ox_send, ox_recv, peer[XP])
    ox_copy.start()

    def tile_of(i):
        return (
            pl.ds(pl.multiple_of((i // HEADS) * QB, QB), QB),
            pl.ds(pl.multiple_of((i % HEADS) * HEAD_DIM, HEAD_DIM), HEAD_DIM),
        )

    def score_step(i, s_ref, j, mx):
        rows, cols = tile_of(i)
        keys = pl.ds(j * KC, KC)
        s = lax.dot_general(k_buf[keys, :], q_buf[rows, cols], NT, preferred_element_type=jnp.float32)
        s = s + bias[keys, rows]
        s_ref[keys, :] = s
        top = jnp.max(s.reshape(KC // 8, 8, QB), axis=0)
        return top if mx is None else jnp.maximum(mx, top)

    def value_step(s_ref, j, m_scaled, total, acc):
        keys = pl.ds(j * KC, KC)
        p = jnp.exp2(s_ref[keys, :] * EXP_SCALE - m_scaled)
        part = jnp.sum(p.reshape(KC // 8, 8, QB), axis=0)
        o = jnp.dot(vt_buf[:, keys], p.astype(jnp.bfloat16), preferred_element_type=jnp.float32)
        return (part, o) if total is None else (total + part, acc + o)

    def ctx_copy(i):
        rows, cols = tile_of(i)
        return rcopy(ctx_own.at[rows, cols], ctx_peer.at[rows, cols], ctx_send.at[i], ctx_recv.at[i], y_peer)

    def tile(i, s_ref, mx, nxt, s_next):
        m_scaled = jnp.max(mx, axis=0, keepdims=True) * EXP_SCALE
        total, acc, mx_next = None, None, None
        for j in range(SEQ // KC):
            mx_next = score_step(nxt, s_next, j, mx_next)
            total, acc = value_step(s_ref, j, m_scaled, total, acc)
        o = acc * (1.0 / jnp.sum(total, axis=0, keepdims=True))
        rows, cols = tile_of(i)
        ctx_own[rows, cols] = jnp.transpose(o).astype(jnp.bfloat16)
        ctx_copy(i).start()
        return mx_next

    def two_tiles(t, mx):
        i = t * 2
        mx = tile(i, s0, mx, i + 1, s1)
        return tile(i + 1, s1, mx, jnp.minimum(i + 2, TILES - 1), s0)

    mx = None
    for j in range(SEQ // KC):
        mx = score_step(0, s0, j, mx)

    def project_out(b):
        rows = pl.ds(pl.multiple_of(b * QB, QB), QB)

        def wait_piece(h, carry):
            ctx_copy(b * HEADS + h).wait_recv()
            return carry

        lax.fori_loop(0, HEADS, wait_piece, 0)

        def out_tile(n, carry):
            cols = pl.ds(pl.multiple_of(n * 256, 256), 256)
            o = jnp.dot(ctx_own[rows, :], wo_buf[own_half, cols], preferred_element_type=jnp.float32) + jnp.dot(
                ctx_peer[rows, :], wo_buf[peer_half, cols], preferred_element_type=jnp.float32
            )
            out_buf[rows, cols] = o.astype(jnp.bfloat16)
            return carry

        lax.fori_loop(0, HID // 256, out_tile, 0)
        pltpu.make_async_copy(out_buf.at[rows], out_hbm.at[rows], out_sem.at[b]).start()

    n_blocks = ROWS // QB
    per_block = HEADS // 2
    mx = lax.fori_loop(0, 3 * per_block, two_tiles, mx)
    ox_copy.wait_recv()
    rows = shard_rows(row_of[XP])
    of_copy = rcopy(wo_buf.at[rows], wo_buf.at[rows], of_send, of_recv, peer[CORE])
    of_copy.start()
    mx = lax.fori_loop(3 * per_block, 4 * per_block, two_tiles, mx)
    wo_local.wait()
    oc_copy.wait_recv()
    of_copy.wait_recv()
    for b in range(n_blocks):
        project_out(b)

    for b in range(n_blocks):
        rows = pl.ds(b * QB, QB)
        pltpu.make_async_copy(out_buf.at[rows], out_hbm.at[rows], out_sem.at[b]).wait()
    for cp in (*tok_copies, *doc_copies, *wx_copies, wc_copy, oc_copy, *wf_copies, *kv_copies, ox_copy, of_copy):
        cp.wait_send()

    def wait_sent(i, carry):
        ctx_copy(i).wait_send()
        return carry

    lax.fori_loop(0, TILES, wait_sent, 0)


def solution(mesh):
    def local_block(tokens, w_qkv, w_out, doc_ids):
        bf16, f32 = jnp.bfloat16, jnp.float32
        dma = pltpu.SemaphoreType.DMA
        any_spec = pl.BlockSpec(memory_space=pl.ANY)
        return pl.pallas_call(
            kernel,
            out_shape=jax.ShapeDtypeStruct(tokens.shape, bf16),
            in_specs=[any_spec] * 4,
            out_specs=any_spec,
            scratch_shapes=[
                pltpu.VMEM((ROWS, HID), bf16),
                pltpu.VMEM((ROWS, HID), bf16),
                pltpu.VMEM((2 * HID, QKV), bf16),
                pltpu.VMEM((2 * HID, HID), bf16),
                pltpu.VMEM((4, 8, 128), jnp.int32),
                pltpu.VMEM((SEQ, 128), jnp.int32),
                pltpu.VMEM((SEQ, ROWS), f32),
                pltpu.VMEM((ROWS, HID), bf16),
                pltpu.VMEM((SEQ, HEAD_DIM), bf16),
                pltpu.VMEM((HEAD_DIM, SEQ), bf16),
                pltpu.VMEM((SEQ, QB), f32),
                pltpu.VMEM((SEQ, QB), f32),
                pltpu.VMEM((ROWS, HID), bf16),
                pltpu.VMEM((ROWS, HID), bf16),
                pltpu.VMEM((ROWS, HID), bf16),
                dma((4,)),
                dma((N_CHUNK,)),
                dma((N_CHUNK,)),
                dma((W_PIECES,)),
                dma((W_PIECES,)),
                dma,
                dma,
                dma((W_PIECES,)),
                dma((W_PIECES,)),
                dma,
                dma,
                dma,
                dma,
                dma,
                dma,
                dma((3,)),
                dma((3,)),
                dma((N_CHUNK, 3, 2)),
                dma((N_CHUNK, 3, 2)),
                dma((TILES,)),
                dma((TILES,)),
                dma((ROWS // QB,)),
            ],
            compiler_params=pltpu.CompilerParams(
                collective_id=0, has_side_effects=True, vmem_limit_bytes=67043328
            ),
        )(tokens, w_qkv, w_out, doc_ids.reshape(8, 128))

    row_spec = P(("data", "row"), "col")
    weight_spec = P("row", "col")
    return jax.shard_map(
        local_block,
        mesh=mesh,
        in_specs=(row_spec, weight_spec, weight_spec, P(("data", "row"))),
        out_specs=row_spec,
        check_vma=False,
    )
```

time: 336 us -> 121 us (0.36)
  waiting for transfers between devices: 160 us -> 0 us
  Pallas kernels: 0 us -> 118 us
  matrix products: 86.4 us -> 0 us
  other arithmetic: 41.6 us -> 0 us
  local copies, waits for them, and re-layouts: 26.8 us -> 3.08 us
  between operations: 13.2 us -> 0.01 us
  blocking collectives: 7.39 us -> 0 us
    all_gather x5 -> x0, waiting for transfers between devices: 158 us -> none  [the longest x1 57.8 us: local_block(): x_panel = lax.all_gather(tokens, 'col', axis=1, tiled=True)]
    pallas_call x0 -> x1, Pallas kernels: none -> 118 us  [local_block(): pl.pallas_call(kernel, out_shape=jax.ShapeDtypeStruct(tokens.shape, bf16)...]
    dot_general x18 -> x0, matrix products: 86.4 us -> none  [the longest x8 42.6 us: attend(): jnp.einsum('qgrk,kgd->qgrd', weights, value_rows, preferred_element_type=...]
    reduce_sum x8 -> x0, other arithmetic: 38.8 us -> none  [attend(): weights = jax.nn.softmax(scores, axis=-1).astype(jnp.bfloat16)]
    all_gather x1 -> x0, blocking collectives: 7.39 us -> none  [local_block(): seg_all = lax.all_gather(doc_ids, 'row', axis=0, tiled=True)]
    dynamic_update_slice x8 -> x0, local copies, waits for them, and re-layouts: 7.06 us -> none  [local_block(): context = lax.map(attend, (q_steps, doc_ids.reshape(n_steps, q_blk)))]
    slice x3 -> x0, local copies, waits for them, and re-layouts: 5.85 us -> none  [the longest x2 5 us: local_block(): qkv_rows[:, :, :group_ratio, :]]
    while x18 -> x0, local copies, waits for them, and re-layouts: 3.91 us -> none  [the longest x2 3.88 us: local_block(): context = lax.map(attend, (q_steps, doc_ids.reshape(n_steps, q_blk)))]
  transfers between devices with their start and end apart: 5 -> 0, of which waited for: 4 -> 0; matrix products, arithmetic and copies ran while one was open for 39% -> 0% of each run, Pallas kernels for 0% -> 0%
where the time goes in v1:
time: 121 us
  Pallas kernels  118 us (98%)
  local copies, waits for them, and re-layouts  3.08 us (3%)
    pallas_call x1, Pallas kernels, local_block(): pl.pallas_call(kernel, out_shape=jax.ShapeDtypeStruct(tokens.shape, bf16)...  118 us
    unnamed x1, local copies, waits for them, and re-layouts  3.08 us

profile of v1, /device:TPU:0, one launch (start us, length us, event | category | flops | bytes accessed | tf_op | source)
XLA Modules:
  0.0 121.1 jit_solution(13518958831338667789)
XLA Ops:
  0.0 118.0 %shard_map.46 = bf16[1024,1024]{1,0:T(8,128)(2,1)} custom-call(bf16[1024,1024]{1,0:T(8,128)(2,1)} %tok_hbm.1, bf16[512,1280]{1,0:T(8,128)(2,1)} %w_hbm.1, bf16[512,1024]{1,0:T(8,128)(2,1)} %wo_hbm.1, s32[8,128]{1,0:T(8,128)} %bitcast.1), custom_call_target="tpu_custom_call" | custom-call | tf_op jit(solution)/shard_map/pallas_call | solution.py:257
  118.0 3.1 %copy.6 = bf16[1024,1024]{1,0:T(8,128)(2,1)} copy(bf16[1024,1024]{1,0:T(8,128)(2,1)} %shard_map.46) | data formatting | bytes 4194304

commit v2 on v1

v2 whole, which is shorter than its diff:
```python
import itertools
import math

import jax
import jax.numpy as jnp
from jax import lax
from jax.experimental import pallas as pl
from jax.experimental.pallas import tpu as pltpu
from jax.sharding import PartitionSpec as P

HEAD_DIM = 128
MESH = pl.DeviceIdType.MESH

ROWS = 1024
HID = 1024
SEQ = 4096
HEADS = 8
QKV = 1280
SHARD = 512
QB = 256
KC = 512
N_STEP = SEQ // KC
CHUNK = 256
N_CHUNK = ROWS // CHUNK
W_PIECES = 4
W_ROWS = SHARD // W_PIECES
N_BLOCK = ROWS // QB
TILES = HEADS * N_BLOCK
N_SEM = 64
CORE, XP, DIAG = 0, 1, 2
EXP_SCALE = math.log2(math.e) / math.sqrt(HEAD_DIM)
NT = (((1,), (1,)), ((), ()))
BF16_MAX = float(jnp.finfo(jnp.bfloat16).max)
F32_MIN = float(jnp.finfo(jnp.float32).min)


def kernel(
    tok_hbm, w_hbm, wo_hbm, doc_hbm, out_hbm,
    tok_own, tok_peer, w_buf, wo_buf, doc_buf, q_buf, qx_buf, k_buf, vt_buf, p0, p1, top_buf,
    ctx_own, ctx_peer, out_buf, loc_sem, send_sem, recv_sem, ctx_send, ctx_recv, out_sem,
):
    d, y, r = lax.axis_index("data"), lax.axis_index("col"), lax.axis_index("row")
    x, core = r // 2, r % 2
    row_of = {CORE: x * 2 + (1 - core), XP: (1 - x) * 2 + core, DIAG: (1 - x) * 2 + (1 - core)}
    y_peer = (d, 1 - y, r)
    peer = {k: (d, y, v) for k, v in row_of.items()}

    barrier = pltpu.get_barrier_semaphore()
    for p in (y_peer, peer[CORE], peer[XP], peer[DIAG]):
        pl.semaphore_signal(barrier, inc=1, device_id=p, device_id_type=MESH)
    pl.semaphore_wait(barrier, 4)

    number = itertools.count()
    sent = []

    def send(src, dst, device):
        i = next(number)
        cp = pltpu.make_async_remote_copy(
            src_ref=src, dst_ref=dst, send_sem=send_sem.at[i], recv_sem=recv_sem.at[i], device_id=device, device_id_type=MESH
        )
        cp.start()
        sent.append(cp)
        return cp

    def local(src, dst, i):
        cp = pltpu.make_async_copy(src, dst, loc_sem.at[i])
        cp.start()
        return cp

    def shard(row, piece=0, size=SHARD):
        return pl.ds(pl.multiple_of(row * SHARD + piece * size, size), size)

    kv_cols, q_cols, k_cols = pl.ds(HID, 2 * HEAD_DIM), pl.ds(0, HID), pl.ds(0, HEAD_DIM)

    tok_in = []
    for c in range(N_CHUNK):
        rows = pl.ds(c * CHUNK, CHUNK)
        tok_in.append(send(tok_hbm.at[rows], tok_peer.at[rows], y_peer))
    wkv_x = send(w_hbm.at[:, kv_cols], w_buf.at[shard(r), kv_cols], peer[XP])
    doc_in = [send(doc_hbm, doc_buf.at[r], peer[k]) for k in (CORE, XP, DIAG)]
    wq_x = [
        send(w_hbm.at[pl.ds(p * W_ROWS, W_ROWS), q_cols], w_buf.at[shard(r, p, W_ROWS), q_cols], peer[XP])
        for p in range(W_PIECES)
    ]
    w_core = send(w_hbm, w_buf.at[shard(r)], peer[CORE])
    wo_core = send(wo_hbm, wo_buf.at[shard(r)], peer[CORE])
    doc_local = local(doc_hbm, doc_buf.at[r], 0)
    w_local = local(w_hbm, w_buf.at[shard(r)], 1)
    tok_local = local(tok_hbm, tok_own, 2)
    wo_local = local(wo_hbm, wo_buf.at[shard(r)], 3)

    doc_local.wait()
    for cp in doc_in:
        cp.wait_recv()
    lane = lax.broadcasted_iota(jnp.int32, (128, 128), 1)

    def as_column(line):
        return jnp.transpose(jnp.broadcast_to(line, (128, 128)))

    def key_mask(i, carry):
        ids = as_column(doc_buf[i // 8, pl.ds(i % 8, 1), :])
        hit = jnp.where(lane < 3, 1 - ids, jnp.where(lane < 6, ids, 0))
        k_buf[pl.ds(pl.multiple_of(i * 128, 128), 128), HEAD_DIM:] = hit.astype(jnp.float32).astype(jnp.bfloat16)
        return carry

    def query_mask(i, carry):
        ids = as_column(doc_buf[r, pl.ds(i, 1), :])
        hit = jnp.where(lane < 3, ids, jnp.where(lane < 6, 1 - ids, 0))
        qx_buf[pl.ds(pl.multiple_of(i * 128, 128), 128), :] = jnp.where(hit == 1, -BF16_MAX, 0.0).astype(jnp.bfloat16)
        return carry

    lax.fori_loop(0, SEQ // 128, key_mask, 0)
    lax.fori_loop(0, ROWS // 128, query_mask, 0)

    own_half = pl.ds(pl.multiple_of(y * HID, HID), HID)
    peer_half = pl.ds(pl.multiple_of((1 - y) * HID, HID), HID)

    def project(rows, cols):
        return jnp.dot(tok_own[rows, :], w_buf[own_half, cols], preferred_element_type=jnp.float32) + jnp.dot(
            tok_peer[rows, :], w_buf[peer_half, cols], preferred_element_type=jnp.float32
        )

    def forward(ref, *index):
        return send(ref.at[index], ref.at[index], peer[CORE])

    k_in, kv_core = [], []

    def keys_of(row, c):
        return pl.ds(pl.multiple_of(row * ROWS + c * CHUNK, CHUNK), CHUNK)

    def project_kv(c):
        tok_in[c].wait_recv()
        kv = project(pl.ds(c * CHUNK, CHUNK), kv_cols).astype(jnp.bfloat16)
        keys = keys_of(r, c)
        k_buf[keys, k_cols] = kv[:, :HEAD_DIM]
        k_in.append([send(k_buf.at[keys, k_cols], k_buf.at[keys, k_cols], peer[XP])])
        vt_buf[:, keys] = jnp.transpose(kv[:, HEAD_DIM:])
        k_in[c].append(send(vt_buf.at[:, keys], vt_buf.at[:, keys], peer[XP]))
        kv_core.append(send(k_buf.at[keys, k_cols], k_buf.at[keys, k_cols], peer[CORE]))
        kv_core.append(send(vt_buf.at[:, keys], vt_buf.at[:, keys], peer[CORE]))

    def forward_kv(c):
        keys = keys_of(row_of[XP], c)
        k_in[c][0].wait_recv()
        kv_core.append(forward(k_buf, keys, k_cols))
        k_in[c][1].wait_recv()
        kv_core.append(forward(vt_buf, slice(None), keys))

    def project_q(c):
        rows = pl.ds(c * CHUNK, CHUNK)

        def q_tile(n, carry):
            cols = pl.ds(pl.multiple_of(n * 256, 256), 256)
            q_buf[rows, cols] = project(rows, cols).astype(jnp.bfloat16)
            return carry

        lax.fori_loop(0, HID // 256, q_tile, 0)

    wkv_x.wait_recv()
    wkv_f = forward(w_buf, shard(row_of[XP]), kv_cols)
    w_local.wait()
    tok_local.wait()
    w_core.wait_recv()
    wkv_f.wait_recv()
    wq_f = []

    def forward_wq(p):
        wq_x[p].wait_recv()
        wq_f.append(forward(w_buf, shard(row_of[XP], p, W_ROWS), q_cols))

    half = SHARD // 2

    def send_wo(p):
        return send(wo_hbm.at[pl.ds(p * half, half)], wo_buf.at[shard(r, p, half)], peer[XP])

    project_kv(0)
    forward_wq(0)
    forward_wq(1)
    project_kv(1)
    forward_wq(2)
    forward_wq(3)
    wo_x = [send_wo(0)]
    for cp in wq_f:
        cp.wait_recv()
    project_q(0)
    project_q(1)
    forward_kv(0)
    forward_kv(1)
    project_kv(2)
    project_q(2)
    forward_kv(2)
    project_kv(3)
    wo_x.append(send_wo(1))
    project_q(3)
    forward_kv(3)
    wo_x[0].wait_recv()
    wo_f = [forward(wo_buf, shard(row_of[XP], 0, half))]
    for cp in kv_core:
        cp.wait_recv()

    def tile_of(i):
        return (
            pl.ds(pl.multiple_of((i // HEADS) * QB, QB), QB),
            pl.ds(pl.multiple_of((i % HEADS) * HEAD_DIM, HEAD_DIM), HEAD_DIM),
        )

    def over_keys(f, a):
        return f(a.reshape(a.shape[0] // 8, 8, QB), axis=0)

    def to_keys(a):
        return jnp.concatenate([a] * (KC // 8), axis=0)

    def score_step(i, slot, p_ref, j, state):
        top, total = state
        rows, cols = tile_of(i)
        keys = pl.ds(j * KC, KC)
        k = k_buf[keys, :]
        q = jnp.concatenate([q_buf[rows, cols], qx_buf[rows, :]], axis=1)
        s = lax.dot_general(k, q, NT, preferred_element_type=jnp.float32)
        new_top = jnp.maximum(top, over_keys(jnp.max, s))
        scaled = new_top * EXP_SCALE
        top_buf[slot, j] = scaled
        p = jnp.exp2(s * EXP_SCALE - to_keys(scaled))
        p_ref[keys, :] = p
        return new_top, total * jnp.exp2(top * EXP_SCALE - scaled) + over_keys(jnp.sum, p)

    def value_step(slot, p_ref, j, lse, acc):
        keys = pl.ds(j * KC, KC)
        weights = p_ref[keys, :] * to_keys(jnp.exp2(top_buf[slot, j] - lse))
        o = jnp.dot(vt_buf[:, keys], weights.astype(jnp.bfloat16), preferred_element_type=jnp.float32)
        return o if acc is None else acc + o

    def ctx_copy(i):
        rows, cols = tile_of(i)
        return pltpu.make_async_remote_copy(
            src_ref=ctx_own.at[rows, cols], dst_ref=ctx_peer.at[rows, cols], send_sem=ctx_send.at[i], recv_sem=ctx_recv.at[i],
            device_id=y_peer, device_id_type=MESH,
        )

    empty = (jnp.full((8, QB), F32_MIN, jnp.float32), jnp.zeros((8, QB), jnp.float32))
    bufs = (p0, p1)

    def tile(i, slot, state, nxt):
        top, total = state
        best = jnp.max(top, axis=0, keepdims=True)
        whole = jnp.sum(total * jnp.exp2((top - best) * EXP_SCALE), axis=0, keepdims=True)
        lse = best * EXP_SCALE + jnp.log2(whole)
        acc, state = None, empty
        for j in range(N_STEP):
            state = score_step(nxt, 1 - slot, bufs[1 - slot], j, state)
            acc = value_step(slot, bufs[slot], j, lse, acc)
        rows, cols = tile_of(i)
        ctx_own[rows, cols] = jnp.transpose(acc).astype(jnp.bfloat16)
        return state

    def two_tiles(t, state):
        i = t * 2
        state = tile(i, 0, state, i + 1)
        state = tile(i + 1, 1, state, jnp.minimum(i + 2, TILES - 1))
        ctx_copy(i).start()
        ctx_copy(i + 1).start()
        return state

    def out_copy(b, n):
        at = (pl.ds(pl.multiple_of(b * QB, QB), QB), pl.ds(pl.multiple_of(n * 256, 256), 256))
        return pltpu.make_async_copy(out_buf.at[at], out_hbm.at[at], out_sem.at[b])

    def project_out(b):
        rows = pl.ds(pl.multiple_of(b * QB, QB), QB)

        def wait_piece(h, carry):
            ctx_copy(b * HEADS + h).wait_recv()
            return carry

        lax.fori_loop(0, HEADS, wait_piece, 0)

        def out_tile(n, carry):
            cols = pl.ds(pl.multiple_of(n * 256, 256), 256)
            o = jnp.dot(ctx_own[rows, :], wo_buf[own_half, cols], preferred_element_type=jnp.float32) + jnp.dot(
                ctx_peer[rows, :], wo_buf[peer_half, cols], preferred_element_type=jnp.float32
            )
            out_buf[rows, cols] = o.astype(jnp.bfloat16)
            return carry

        lax.fori_loop(0, HID // 256, out_tile, 0)
        out = pltpu.make_async_copy(out_buf.at[rows], out_hbm.at[rows], out_sem.at[b])
        out.start()

    state = empty
    for j in range(N_STEP):
        state = score_step(0, 0, p0, j, state)

    pairs = HEADS // 2
    state = lax.fori_loop(0, 2 * pairs, two_tiles, state)
    wo_x[1].wait_recv()
    wo_f.append(forward(wo_buf, shard(row_of[XP], 1, half)))
    wo_local.wait()
    wo_core.wait_recv()
    for cp in wo_f:
        cp.wait_recv()

    def later_block(b, state):
        project_out(b - 2)
        return lax.fori_loop(b * pairs, (b + 1) * pairs, two_tiles, state)

    lax.fori_loop(2, N_BLOCK, later_block, state)

    def last_block(b, carry):
        project_out(b)
        return carry

    lax.fori_loop(N_BLOCK - 2, N_BLOCK, last_block, 0)

    def wait_out(b, carry):
        rows = pl.ds(pl.multiple_of(b * QB, QB), QB)
        pltpu.make_async_copy(out_buf.at[rows], out_hbm.at[rows], out_sem.at[b]).wait()
        return carry

    lax.fori_loop(0, N_BLOCK, wait_out, 0)
    for cp in sent:
        cp.wait_send()

    def wait_sent(i, carry):
        ctx_copy(i).wait_send()
        return carry

    lax.fori_loop(0, TILES, wait_sent, 0)
    assert next(number) <= N_SEM


def solution(mesh):
    def local_block(tokens, w_qkv, w_out, doc_ids):
        bf16, f32 = jnp.bfloat16, jnp.float32
        dma = pltpu.SemaphoreType.DMA
        any_spec = pl.BlockSpec(memory_space=pl.ANY)
        return pl.pallas_call(
            kernel,
            out_shape=jax.ShapeDtypeStruct(tokens.shape, bf16),
            in_specs=[any_spec] * 4,
            out_specs=any_spec,
            scratch_shapes=[
                pltpu.VMEM((ROWS, HID), bf16),
                pltpu.VMEM((ROWS, HID), bf16),
                pltpu.VMEM((2 * HID, QKV), bf16),
                pltpu.VMEM((2 * HID, HID), bf16),
                pltpu.VMEM((4, 8, 128), jnp.int32),
                pltpu.VMEM((ROWS, HID), bf16),
                pltpu.VMEM((ROWS, 128), bf16),
                pltpu.VMEM((SEQ, 2 * HEAD_DIM), bf16),
                pltpu.VMEM((HEAD_DIM, SEQ), bf16),
                pltpu.VMEM((SEQ, QB), f32),
                pltpu.VMEM((SEQ, QB), f32),
                pltpu.VMEM((2, N_STEP, 8, QB), f32),
                pltpu.VMEM((ROWS, HID), bf16),
                pltpu.VMEM((ROWS, HID), bf16),
                pltpu.VMEM((ROWS, HID), bf16),
                dma((4,)),
                dma((N_SEM,)),
                dma((N_SEM,)),
                dma((TILES,)),
                dma((TILES,)),
                dma((N_BLOCK,)),
            ],
            compiler_params=pltpu.CompilerParams(
                collective_id=0, has_side_effects=True, vmem_limit_bytes=67043328
            ),
        )(tokens, w_qkv, w_out, doc_ids.reshape(8, 128))

    row_spec = P(("data", "row"), "col")
    weight_spec = P("row", "col")
    return jax.shard_map(
        local_block,
        mesh=mesh,
        in_specs=(row_spec, weight_spec, weight_spec, P(("data", "row"))),
        out_specs=row_spec,
        check_vma=False,
    )
```

time: 121 us -> 132 us (1.091)
  Pallas kernels: 118 us -> 128 us
    pallas_call x1, Pallas kernels: 118 us -> 128 us  [local_block(): pl.pallas_call(kernel, out_shape=jax.ShapeDtypeStruct(tokens.shape, bf16)...]
where the time goes in v2:
time: 132 us
  Pallas kernels  128 us (97%)
  local copies, waits for them, and re-layouts  3.08 us (2%)
    pallas_call x1, Pallas kernels, local_block(): pl.pallas_call(kernel, out_shape=jax.ShapeDtypeStruct(tokens.shape, bf16)...  128 us
    unnamed x1, local copies, waits for them, and re-layouts  3.08 us

profile of v2, /device:TPU:0, one launch (start us, length us, event | category | flops | bytes accessed | tf_op | source)
XLA Modules:
  0.0 131.6 jit_solution(18167568458359271759)
XLA Ops:
  0.0 128.5 %shard_map.46 = bf16[1024,1024]{1,0:T(8,128)(2,1)} custom-call(bf16[1024,1024]{1,0:T(8,128)(2,1)} %tok_hbm.1, bf16[512,1280]{1,0:T(8,128)(2,1)} %w_hbm.1, bf16[512,1024]{1,0:T(8,128)(2,1)} %wo_hbm.1, s32[8,128]{1,0:T(8,128)} %bitcast.1), custom_call_target="tpu_custom_call" | custom-call | tf_op jit(solution)/shard_map/pallas_call | solution.py:336
  128.5 3.1 %copy.6 = bf16[1024,1024]{1,0:T(8,128)(2,1)} copy(bf16[1024,1024]{1,0:T(8,128)(2,1)} %shard_map.46) | data formatting | bytes 4194304

commit v3 on v2

v3 whole, which is shorter than its diff:
```python
import itertools
import math

import jax
import jax.numpy as jnp
from jax import lax
from jax.experimental import pallas as pl
from jax.experimental.pallas import tpu as pltpu
from jax.sharding import PartitionSpec as P

HEAD_DIM = 128
MESH = pl.DeviceIdType.MESH

ROWS = 1024
HID = 1024
SEQ = 4096
HEADS = 8
QKV = 1280
SHARD = 512
QB = 256
KC = 1024
GROUP = 128
N_GROUP = KC // GROUP
N_STEP = SEQ // KC
CHUNKS = ((0, 256), (256, 256), (512, 256), (768, 128), (896, 128))
W_PIECES = 4
W_ROWS = SHARD // W_PIECES
N_BLOCK = ROWS // QB
TILES = HEADS * N_BLOCK
SLOTS = 8
N_SEM = 64
CORE, XP, DIAG = 0, 1, 2
EXP_SCALE = math.log2(math.e) / math.sqrt(HEAD_DIM)
NT = (((1,), (1,)), ((), ()))
BF16_MAX = float(jnp.finfo(jnp.bfloat16).max)
F32_MIN = float(jnp.finfo(jnp.float32).min)


def kernel(
    tok_hbm, w_hbm, wo_hbm, doc_hbm, out_hbm,
    tok_own, tok_peer, w_buf, wo_buf, doc_buf, q_buf, qx_buf, k_buf, vt_buf, p_buf, top_buf, state_buf,
    ctx_own, ctx_peer, loc_sem, send_sem, recv_sem, ctx_send, ctx_recv, out_sem,
):
    d, y, r = lax.axis_index("data"), lax.axis_index("col"), lax.axis_index("row")
    x, core = r // 2, r % 2
    row_of = {CORE: x * 2 + (1 - core), XP: (1 - x) * 2 + core, DIAG: (1 - x) * 2 + (1 - core)}
    y_peer = (d, 1 - y, r)
    peer = {k: (d, y, v) for k, v in row_of.items()}
    out_buf = tok_own

    barrier = pltpu.get_barrier_semaphore()
    for p in (y_peer, peer[CORE], peer[XP], peer[DIAG]):
        pl.semaphore_signal(barrier, inc=1, device_id=p, device_id_type=MESH)
    pl.semaphore_wait(barrier, 4)

    number = itertools.count()
    sent = []

    def send(src, dst, device):
        i = next(number)
        cp = pltpu.make_async_remote_copy(
            src_ref=src, dst_ref=dst, send_sem=send_sem.at[i], recv_sem=recv_sem.at[i], device_id=device, device_id_type=MESH
        )
        cp.start()
        sent.append(cp)
        return cp

    def local(src, dst, i):
        cp = pltpu.make_async_copy(src, dst, loc_sem.at[i])
        cp.start()
        return cp

    def shard(row, piece=0, size=SHARD):
        return pl.ds(pl.multiple_of(row * SHARD + piece * size, size), size)

    kv_cols, q_cols, k_cols = pl.ds(HID, 2 * HEAD_DIM), pl.ds(0, HID), pl.ds(0, HEAD_DIM)

    tok_in = []
    for first, size in CHUNKS:
        rows = pl.ds(first, size)
        tok_in.append(send(tok_hbm.at[rows], tok_peer.at[rows], y_peer))
    wkv_x = send(w_hbm.at[:, kv_cols], w_buf.at[shard(r), kv_cols], peer[XP])
    doc_in = [send(doc_hbm, doc_buf.at[r], peer[k]) for k in (CORE, XP, DIAG)]
    wq_x = [
        send(w_hbm.at[pl.ds(p * W_ROWS, W_ROWS), q_cols], w_buf.at[shard(r, p, W_ROWS), q_cols], peer[XP])
        for p in range(W_PIECES)
    ]
    w_core = send(w_hbm, w_buf.at[shard(r)], peer[CORE])
    wo_core = send(wo_hbm, wo_buf.at[shard(r)], peer[CORE])
    doc_local = local(doc_hbm, doc_buf.at[r], 0)
    w_local = local(w_hbm, w_buf.at[shard(r)], 1)
    tok_local = local(tok_hbm, tok_own, 2)
    wo_local = local(wo_hbm, wo_buf.at[shard(r)], 3)

    doc_local.wait()
    for cp in doc_in:
        cp.wait_recv()
    lane = lax.broadcasted_iota(jnp.int32, (128, 128), 1)

    def as_column(line):
        return jnp.transpose(jnp.broadcast_to(line, (128, 128)))

    def key_mask(place):
        def line_mask(i, carry):
            part, line, first = place(i)
            ids = as_column(doc_buf[part, pl.ds(line, 1), :])
            hit = jnp.where(lane < 3, 1 - ids, jnp.where(lane < 6, ids, 0))
            k_buf[pl.ds(pl.multiple_of(first, 128), 128), HEAD_DIM:] = hit.astype(jnp.float32).astype(jnp.bfloat16)
            return carry

        return line_mask

    def query_mask(i, carry):
        ids = as_column(doc_buf[r, pl.ds(i, 1), :])
        hit = jnp.where(lane < 3, ids, jnp.where(lane < 6, 1 - ids, 0))
        qx_buf[pl.ds(pl.multiple_of(i * 128, 128), 128), :] = jnp.where(hit == 1, -BF16_MAX, 0.0).astype(jnp.bfloat16)
        return carry

    wide = key_mask(lambda i: (i // 6, i % 6, (i % 6) // 2 * 1024 + i // 6 * 256 + i % 2 * 128))
    lax.fori_loop(0, 24, wide, 0)
    narrow = key_mask(lambda i: (i // 2, 6 + i % 2, 3072 + i % 2 * 512 + i // 2 * 128))
    lax.fori_loop(0, 8, narrow, 0)
    lax.fori_loop(0, ROWS // 128, query_mask, 0)

    own_half = pl.ds(pl.multiple_of(y * HID, HID), HID)
    peer_half = pl.ds(pl.multiple_of((1 - y) * HID, HID), HID)

    def project(rows, cols):
        return jnp.dot(tok_own[rows, :], w_buf[own_half, cols], preferred_element_type=jnp.float32) + jnp.dot(
            tok_peer[rows, :], w_buf[peer_half, cols], preferred_element_type=jnp.float32
        )

    def forward(ref, *index):
        return send(ref.at[index], ref.at[index], peer[CORE])

    k_in, kv_core = [], [[] for _ in CHUNKS]

    def keys_of(row, c):
        first, size = CHUNKS[c]
        return pl.ds(pl.multiple_of(first * 4 + row * size, size), size)

    def project_kv(c):
        tok_in[c].wait_recv()
        kv = project(pl.ds(*CHUNKS[c]), kv_cols).astype(jnp.bfloat16)
        keys = keys_of(r, c)
        k_buf[keys, k_cols] = kv[:, :HEAD_DIM]
        k_in.append([send(k_buf.at[keys, k_cols], k_buf.at[keys, k_cols], peer[XP])])
        vt_buf[:, keys] = jnp.transpose(kv[:, HEAD_DIM:])
        k_in[c].append(send(vt_buf.at[:, keys], vt_buf.at[:, keys], peer[XP]))
        kv_core[c].append(send(k_buf.at[keys, k_cols], k_buf.at[keys, k_cols], peer[CORE]))
        kv_core[c].append(send(vt_buf.at[:, keys], vt_buf.at[:, keys], peer[CORE]))

    def forward_kv(c):
        keys = keys_of(row_of[XP], c)
        k_in[c][0].wait_recv()
        kv_core[c].append(forward(k_buf, keys, k_cols))
        k_in[c][1].wait_recv()
        kv_core[c].append(forward(vt_buf, slice(None), keys))

    def wait_kv(c):
        for cp in kv_core[c]:
            cp.wait_recv()

    def project_q(c):
        rows = pl.ds(c * QB, QB)

        def q_tile(n, carry):
            cols = pl.ds(pl.multiple_of(n * 256, 256), 256)
            q_buf[rows, cols] = project(rows, cols).astype(jnp.bfloat16)
            return carry

        lax.fori_loop(0, HID // 256, q_tile, 0)

    wkv_x.wait_recv()
    wkv_f = forward(w_buf, shard(row_of[XP]), kv_cols)
    w_local.wait()
    tok_local.wait()
    w_core.wait_recv()
    wkv_f.wait_recv()
    wq_f = []

    def forward_wq(p):
        wq_x[p].wait_recv()
        wq_f.append(forward(w_buf, shard(row_of[XP], p, W_ROWS), q_cols))

    half = SHARD // 2

    def send_wo(p):
        return send(wo_hbm.at[pl.ds(p * half, half)], wo_buf.at[shard(r, p, half)], peer[XP])

    def tile_of(i):
        return (
            pl.ds(pl.multiple_of((i // HEADS) * QB, QB), QB),
            pl.ds(pl.multiple_of((i % HEADS) * HEAD_DIM, HEAD_DIM), HEAD_DIM),
        )

    def over_keys(f, a):
        return f(a.reshape(a.shape[0] // 8, 8, QB), axis=0)

    def to_keys(a):
        return jnp.concatenate([a] * (GROUP // 8), axis=0)

    def score_step(i, slot, j, state):
        top, total = state
        rows, cols = tile_of(i)
        q = jnp.concatenate([q_buf[rows, cols], qx_buf[rows, :]], axis=1)
        s = lax.dot_general(k_buf[pl.ds(j * KC, KC), :], q, NT, preferred_element_type=jnp.float32)
        for g in range(N_GROUP):
            part = s[g * GROUP : (g + 1) * GROUP]
            new_top = jnp.maximum(top, over_keys(jnp.max, part))
            scaled = new_top * EXP_SCALE
            top_buf[slot, j * N_GROUP + g] = scaled
            p = jnp.exp2(part * EXP_SCALE - to_keys(scaled))
            p_buf[slot, pl.ds(j * KC + g * GROUP, GROUP), :] = p
            total = total * jnp.exp2(top * EXP_SCALE - scaled) + over_keys(jnp.sum, p)
            top = new_top
        return top, total

    def value_step(slot, j, lse, acc):
        keys = pl.ds(j * KC, KC)
        factor = [to_keys(jnp.exp2(top_buf[slot, j * N_GROUP + g] - lse)) for g in range(N_GROUP)]
        weights = p_buf[slot, keys, :] * jnp.concatenate(factor, axis=0)
        o = jnp.dot(vt_buf[:, keys], weights.astype(jnp.bfloat16), preferred_element_type=jnp.float32)
        return o if acc is None else acc + o

    def ctx_copy(i):
        rows, cols = tile_of(i)
        return pltpu.make_async_remote_copy(
            src_ref=ctx_own.at[rows, cols], dst_ref=ctx_peer.at[rows, cols], send_sem=ctx_send.at[i], recv_sem=ctx_recv.at[i],
            device_id=y_peer, device_id_type=MESH,
        )

    empty = (jnp.full((8, QB), F32_MIN, jnp.float32), jnp.zeros((8, QB), jnp.float32))

    def load_state(slot):
        return state_buf[slot, 0], state_buf[slot, 1]

    def prefetch(*steps):
        def one(slot, carry):
            state = load_state(slot) if steps[0] else empty
            for j in steps:
                state = score_step(slot, slot, j, state)
            state_buf[slot, 0], state_buf[slot, 1] = state
            return carry

        lax.fori_loop(0, SLOTS, one, 0)

    def tile(i, slot, state, nxt=None, nxt_slot=None, nxt_state=None, nxt_steps=()):
        top, total = state
        best = jnp.max(top, axis=0, keepdims=True)
        whole = jnp.sum(total * jnp.exp2((top - best) * EXP_SCALE), axis=0, keepdims=True)
        lse = best * EXP_SCALE + jnp.log2(whole)
        acc = None
        steps = list(nxt_steps)
        for j in range(N_STEP):
            if steps:
                nxt_state = score_step(nxt, nxt_slot, steps.pop(0), nxt_state)
            acc = value_step(slot, j, lse, acc)
        rows, cols = tile_of(i)
        ctx_own[rows, cols] = jnp.transpose(acc).astype(jnp.bfloat16)
        return nxt_state

    every = range(N_STEP)

    def two_tiles(t, state):
        i = t * 2
        state = tile(i, 0, state, i + 1, 1, empty, every)
        state = tile(i + 1, 1, state, i + 2, 0, empty, every)
        ctx_copy(i).start()
        ctx_copy(i + 1).start()
        return state

    def project_out(b):
        rows = pl.ds(pl.multiple_of(b * QB, QB), QB)

        def wait_piece(h, carry):
            ctx_copy(b * HEADS + h).wait_recv()
            return carry

        lax.fori_loop(0, HEADS, wait_piece, 0)

        def out_tile(n, carry):
            cols = pl.ds(pl.multiple_of(n * 256, 256), 256)
            o = jnp.dot(ctx_own[rows, :], wo_buf[own_half, cols], preferred_element_type=jnp.float32) + jnp.dot(
                ctx_peer[rows, :], wo_buf[peer_half, cols], preferred_element_type=jnp.float32
            )
            out_buf[rows, cols] = o.astype(jnp.bfloat16)
            return carry

        lax.fori_loop(0, HID // 256, out_tile, 0)
        out = pltpu.make_async_copy(out_buf.at[rows], out_hbm.at[rows], out_sem.at[b])
        out.start()

    project_kv(0)
    forward_wq(0)
    forward_wq(1)
    project_kv(1)
    forward_wq(2)
    forward_wq(3)
    for cp in wq_f:
        cp.wait_recv()
    project_q(0)
    project_q(1)
    forward_kv(0)
    forward_kv(1)
    project_kv(2)
    project_q(2)
    for c in (0, 1):
        wait_kv(c)
    prefetch(0, 1)
    forward_kv(2)
    project_kv(3)
    wait_kv(2)
    prefetch(2)
    forward_kv(3)
    project_kv(4)
    wo_x = [send_wo(0), send_wo(1)]
    project_q(3)
    forward_kv(4)
    for c in (3, 4):
        wait_kv(c)

    last = N_STEP - 1
    state = score_step(0, 0, last, load_state(0))
    for i in range(SLOTS):
        if i + 1 < SLOTS:
            state = tile(i, i, state, i + 1, i + 1, load_state(i + 1), (last,))
        else:
            state = tile(i, i, state, i + 1, 0, empty, every)
        if i % 2:
            ctx_copy(i - 1).start()
            ctx_copy(i).start()

    pairs = HEADS // 2
    state = lax.fori_loop(pairs, 2 * pairs, two_tiles, state)
    wo_f = []
    for p in (0, 1):
        wo_x[p].wait_recv()
        wo_f.append(forward(wo_buf, shard(row_of[XP], p, half)))

    state = lax.fori_loop(2 * pairs, 3 * pairs, two_tiles, state)
    wo_local.wait()
    wo_core.wait_recv()
    for cp in wo_f:
        cp.wait_recv()
    project_out(0)
    state = lax.fori_loop(3 * pairs, 4 * pairs - 1, two_tiles, state)
    state = tile(TILES - 2, 0, state, TILES - 1, 1, empty, every)
    ctx_copy(TILES - 2).start()
    tile(TILES - 1, 1, state)
    ctx_copy(TILES - 1).start()

    def last_block(b, carry):
        project_out(b)
        return carry

    lax.fori_loop(1, N_BLOCK, last_block, 0)

    def wait_out(b, carry):
        rows = pl.ds(pl.multiple_of(b * QB, QB), QB)
        pltpu.make_async_copy(out_buf.at[rows], out_hbm.at[rows], out_sem.at[b]).wait()
        return carry

    lax.fori_loop(0, N_BLOCK, wait_out, 0)
    for cp in sent:
        cp.wait_send()

    def wait_sent(i, carry):
        ctx_copy(i).wait_send()
        return carry

    lax.fori_loop(0, TILES, wait_sent, 0)
    assert next(number) <= N_SEM


def solution(mesh):
    def local_block(tokens, w_qkv, w_out, doc_ids):
        bf16, f32 = jnp.bfloat16, jnp.float32
        dma = pltpu.SemaphoreType.DMA
        any_spec = pl.BlockSpec(memory_space=pl.ANY)
        return pl.pallas_call(
            kernel,
            out_shape=jax.ShapeDtypeStruct(tokens.shape, bf16),
            in_specs=[any_spec] * 4,
            out_specs=any_spec,
            scratch_shapes=[
                pltpu.VMEM((ROWS, HID), bf16),
                pltpu.VMEM((ROWS, HID), bf16),
                pltpu.VMEM((2 * HID, QKV), bf16),
                pltpu.VMEM((2 * HID, HID), bf16),
                pltpu.VMEM((4, 8, 128), jnp.int32),
                pltpu.VMEM((ROWS, HID), bf16),
                pltpu.VMEM((ROWS, 128), bf16),
                pltpu.VMEM((SEQ, 2 * HEAD_DIM), bf16),
                pltpu.VMEM((HEAD_DIM, SEQ), bf16),
                pltpu.VMEM((SLOTS, SEQ, QB), f32),
                pltpu.VMEM((SLOTS, SEQ // GROUP, 8, QB), f32),
                pltpu.VMEM((SLOTS, 2, 8, QB), f32),
                pltpu.VMEM((ROWS, HID), bf16),
                pltpu.VMEM((ROWS, HID), bf16),
                dma((4,)),
                dma((N_SEM,)),
                dma((N_SEM,)),
                dma((TILES,)),
                dma((TILES,)),
                dma((N_BLOCK,)),
            ],
            compiler_params=pltpu.CompilerParams(
                collective_id=0, has_side_effects=True, vmem_limit_bytes=67043328
            ),
        )(tokens, w_qkv, w_out, doc_ids.reshape(8, 128))

    row_spec = P(("data", "row"), "col")
    weight_spec = P("row", "col")
    return jax.shard_map(
        local_block,
        mesh=mesh,
        in_specs=(row_spec, weight_spec, weight_spec, P(("data", "row"))),
        out_specs=row_spec,
        check_vma=False,
    )
```

time: 132 us -> 117 us (0.89)
  Pallas kernels: 128 us -> 113 us
    pallas_call x1, Pallas kernels: 128 us -> 113 us  [local_block(): pl.pallas_call(kernel, out_shape=jax.ShapeDtypeStruct(tokens.shape, bf16)...]
where the time goes in v3:
time: 117 us
  Pallas kernels  113 us (97%)
  local copies, waits for them, and re-layouts  3.08 us (3%)
    pallas_call x1, Pallas kernels, local_block(): pl.pallas_call(kernel, out_shape=jax.ShapeDtypeStruct(tokens.shape, bf16)...  113 us
    unnamed x1, local copies, waits for them, and re-layouts  3.08 us

profile of v3, /device:TPU:0, one launch (start us, length us, event | category | flops | bytes accessed | tf_op | source)
XLA Modules:
  0.0 116.5 jit_solution(8184634705376227821)
XLA Ops:
  0.0 113.5 %shard_map.46 = bf16[1024,1024]{1,0:T(8,128)(2,1)} custom-call(bf16[1024,1024]{1,0:T(8,128)(2,1)} %tok_hbm.1, bf16[512,1280]{1,0:T(8,128)(2,1)} %w_hbm.1, bf16[512,1024]{1,0:T(8,128)(2,1)} %wo_hbm.1, s32[8,128]{1,0:T(8,128)} %bitcast.1), custom_call_target="tpu_custom_call" | custom-call | tf_op jit(solution)/shard_map/pallas_call | solution.py:381
  113.5 3.1 %copy.6 = bf16[1024,1024]{1,0:T(8,128)(2,1)} copy(bf16[1024,1024]{1,0:T(8,128)(2,1)} %shard_map.46) | data formatting | bytes 4194304

commit v4 on v3

--- a/solution.py
+++ b/solution.py
@@ -38,7 +38,7 @@
 
 def kernel(
     tok_hbm, w_hbm, wo_hbm, doc_hbm, out_hbm,
-    tok_own, tok_peer, w_buf, wo_buf, doc_buf, q_buf, qx_buf, k_buf, vt_buf, p_buf, top_buf, state_buf,
+    tok_own, tok_peer, w_buf, wo_buf, doc_buf, q_buf, qx_buf, k_buf, kx_buf, vw_buf, vn_buf, p_buf, top_buf, state_buf,
     ctx_own, ctx_peer, loc_sem, send_sem, recv_sem, ctx_send, ctx_recv, out_sem,
 ):
     d, y, r = lax.axis_index("data"), lax.axis_index("col"), lax.axis_index("row")
@@ -73,7 +73,7 @@
     def shard(row, piece=0, size=SHARD):
         return pl.ds(pl.multiple_of(row * SHARD + piece * size, size), size)
 
-    kv_cols, q_cols, k_cols = pl.ds(HID, 2 * HEAD_DIM), pl.ds(0, HID), pl.ds(0, HEAD_DIM)
+    kv_cols, q_cols = pl.ds(HID, 2 * HEAD_DIM), pl.ds(0, HID)
 
     tok_in = []
     for first, size in CHUNKS:
@@ -105,7 +105,7 @@
             part, line, first = place(i)
             ids = as_column(doc_buf[part, pl.ds(line, 1), :])
             hit = jnp.where(lane < 3, 1 - ids, jnp.where(lane < 6, ids, 0))
-            k_buf[pl.ds(pl.multiple_of(first, 128), 128), HEAD_DIM:] = hit.astype(jnp.float32).astype(jnp.bfloat16)
+            kx_buf[pl.ds(pl.multiple_of(first, 128), 128), :] = hit.astype(jnp.float32).astype(jnp.bfloat16)
             return carry
 
         return line_mask
@@ -137,25 +137,24 @@
 
     def keys_of(row, c):
         first, size = CHUNKS[c]
-        return pl.ds(pl.multiple_of(first * 4 + row * size, size), size)
+        values = vw_buf.at[c * 4 + row] if size == 256 else vn_buf.at[(c - N_STEP + 1) * 4 + row]
+        return k_buf.at[pl.ds(pl.multiple_of(first * 4 + row * size, size), size)], values
 
     def project_kv(c):
         tok_in[c].wait_recv()
         kv = project(pl.ds(*CHUNKS[c]), kv_cols).astype(jnp.bfloat16)
-        keys = keys_of(r, c)
-        k_buf[keys, k_cols] = kv[:, :HEAD_DIM]
-        k_in.append([send(k_buf.at[keys, k_cols], k_buf.at[keys, k_cols], peer[XP])])
-        vt_buf[:, keys] = jnp.transpose(kv[:, HEAD_DIM:])
-        k_in[c].append(send(vt_buf.at[:, keys], vt_buf.at[:, keys], peer[XP]))
-        kv_core[c].append(send(k_buf.at[keys, k_cols], k_buf.at[keys, k_cols], peer[CORE]))
-        kv_core[c].append(send(vt_buf.at[:, keys], vt_buf.at[:, keys], peer[CORE]))
+        keys, values = keys_of(r, c)
+        keys[...] = kv[:, :HEAD_DIM]
+        k_in.append([send(keys, keys, peer[XP])])
+        values[...] = jnp.transpose(kv[:, HEAD_DIM:])
+        k_in[c].append(send(values, values, peer[XP]))
+        kv_core[c].append(send(keys, keys, peer[CORE]))
+        kv_core[c].append(send(values, values, peer[CORE]))
 
     def forward_kv(c):
-        keys = keys_of(row_of[XP], c)
-        k_in[c][0].wait_recv()
-        kv_core[c].append(forward(k_buf, keys, k_cols))
-        k_in[c][1].wait_recv()
-        kv_core[c].append(forward(vt_buf, slice(None), keys))
+        for ref, cp in zip(keys_of(row_of[XP], c), k_in[c]):
+            cp.wait_recv()
+            kv_core[c].append(send(ref, ref, peer[CORE]))
 
     def wait_kv(c):
         for cp in kv_core[c]:
@@ -204,7 +203,8 @@
         top, total = state
         rows, cols = tile_of(i)
         q = jnp.concatenate([q_buf[rows, cols], qx_buf[rows, :]], axis=1)
-        s = lax.dot_general(k_buf[pl.ds(j * KC, KC), :], q, NT, preferred_element_type=jnp.float32)
+        k = jnp.concatenate([k_buf[pl.ds(j * KC, KC), :], kx_buf[pl.ds(j * KC, KC), :]], axis=1)
+        s = lax.dot_general(k, q, NT, preferred_element_type=jnp.float32)
         for g in range(N_GROUP):
             part = s[g * GROUP : (g + 1) * GROUP]
             new_top = jnp.maximum(top, over_keys(jnp.max, part))
@@ -220,13 +220,13 @@
         keys = pl.ds(j * KC, KC)
         factor = [to_keys(jnp.exp2(top_buf[slot, j * N_GROUP + g] - lse)) for g in range(N_GROUP)]
         weights = p_buf[slot, keys, :] * jnp.concatenate(factor, axis=0)
-        o = jnp.dot(vt_buf[:, keys], weights.astype(jnp.bfloat16), preferred_element_type=jnp.float32)
+        parts = [vw_buf[j * 4 + i] for i in range(4)] if j + 1 < N_STEP else [vn_buf[i] for i in range(8)]
+        o = jnp.dot(jnp.concatenate(parts, axis=1), weights.astype(jnp.bfloat16), preferred_element_type=jnp.float32)
         return o if acc is None else acc + o
 
     def ctx_copy(i):
-        rows, cols = tile_of(i)
         return pltpu.make_async_remote_copy(
-            src_ref=ctx_own.at[rows, cols], dst_ref=ctx_peer.at[rows, cols], send_sem=ctx_send.at[i], recv_sem=ctx_recv.at[i],
+            src_ref=ctx_own.at[i], dst_ref=ctx_peer.at[i], send_sem=ctx_send.at[i], recv_sem=ctx_recv.at[i],
             device_id=y_peer, device_id_type=MESH,
         )
 
@@ -256,8 +256,7 @@
             if steps:
                 nxt_state = score_step(nxt, nxt_slot, steps.pop(0), nxt_state)
             acc = value_step(slot, j, lse, acc)
-        rows, cols = tile_of(i)
-        ctx_own[rows, cols] = jnp.transpose(acc).astype(jnp.bfloat16)
+        ctx_own[i] = jnp.transpose(acc).astype(jnp.bfloat16)
         return nxt_state
 
     every = range(N_STEP)
@@ -281,8 +280,9 @@
 
         def out_tile(n, carry):
             cols = pl.ds(pl.multiple_of(n * 256, 256), 256)
-            o = jnp.dot(ctx_own[rows, :], wo_buf[own_half, cols], preferred_element_type=jnp.float32) + jnp.dot(
-                ctx_peer[rows, :], wo_buf[peer_half, cols], preferred_element_type=jnp.float32
+            own, other = (jnp.concatenate([ref[b * HEADS + h] for h in range(HEADS)], axis=1) for ref in (ctx_own, ctx_peer))
+            o = jnp.dot(own, wo_buf[own_half, cols], preferred_element_type=jnp.float32) + jnp.dot(
+                other, wo_buf[peer_half, cols], preferred_element_type=jnp.float32
             )
             out_buf[rows, cols] = o.astype(jnp.bfloat16)
             return carry
@@ -334,27 +334,30 @@
     pairs = HEADS // 2
     state = lax.fori_loop(pairs, 2 * pairs, two_tiles, state)
     wo_f = []
-    for p in (0, 1):
+
+    def forward_wo(p):
         wo_x[p].wait_recv()
         wo_f.append(forward(wo_buf, shard(row_of[XP], p, half)))
 
+    forward_wo(0)
     state = lax.fori_loop(2 * pairs, 3 * pairs, two_tiles, state)
-    wo_local.wait()
-    wo_core.wait_recv()
-    for cp in wo_f:
-        cp.wait_recv()
-    project_out(0)
+    forward_wo(1)
     state = lax.fori_loop(3 * pairs, 4 * pairs - 1, two_tiles, state)
     state = tile(TILES - 2, 0, state, TILES - 1, 1, empty, every)
     ctx_copy(TILES - 2).start()
     tile(TILES - 1, 1, state)
     ctx_copy(TILES - 1).start()
 
+    wo_local.wait()
+    wo_core.wait_recv()
+    for cp in wo_f:
+        cp.wait_recv()
+
     def last_block(b, carry):
         project_out(b)
         return carry
 
-    lax.fori_loop(1, N_BLOCK, last_block, 0)
+    lax.fori_loop(0, N_BLOCK, last_block, 0)
 
     def wait_out(b, carry):
         rows = pl.ds(pl.multiple_of(b * QB, QB), QB)
@@ -391,13 +394,15 @@
                 pltpu.VMEM((4, 8, 128), jnp.int32),
                 pltpu.VMEM((ROWS, HID), bf16),
                 pltpu.VMEM((ROWS, 128), bf16),
-                pltpu.VMEM((SEQ, 2 * HEAD_DIM), bf16),
-                pltpu.VMEM((HEAD_DIM, SEQ), bf16),
+                pltpu.VMEM((SEQ, HEAD_DIM), bf16),
+                pltpu.VMEM((SEQ, HEAD_DIM), bf16),
+                pltpu.VMEM((12, HEAD_DIM, 256), bf16),
+                pltpu.VMEM((8, HEAD_DIM, 128), bf16),
                 pltpu.VMEM((SLOTS, SEQ, QB), f32),
                 pltpu.VMEM((SLOTS, SEQ // GROUP, 8, QB), f32),
                 pltpu.VMEM((SLOTS, 2, 8, QB), f32),
-                pltpu.VMEM((ROWS, HID), bf16),
-                pltpu.VMEM((ROWS, HID), bf16),
+                pltpu.VMEM((TILES, QB, HEAD_DIM), bf16),
+                pltpu.VMEM((TILES, QB, HEAD_DIM), bf16),
                 dma((4,)),
                 dma((N_SEM,)),
                 dma((N_SEM,)),

time: 117 us -> 115 us (0.983)
  Pallas kernels: 113 us -> 111 us
    pallas_call x1, Pallas kernels: 113 us -> 111 us  [local_block(): pl.pallas_call(kernel, out_shape=jax.ShapeDtypeStruct(tokens.shape, bf16)...]
where the time goes in v4:
time: 115 us
  Pallas kernels  111 us (97%)
  local copies, waits for them, and re-layouts  3.08 us (3%)
    pallas_call x1, Pallas kernels, local_block(): pl.pallas_call(kernel, out_shape=jax.ShapeDtypeStruct(tokens.shape, bf16)...  111 us
    unnamed x1, local copies, waits for them, and re-layouts  3.08 us

profile of v4, /device:TPU:0, one launch (start us, length us, event | category | flops | bytes accessed | tf_op | source)
XLA Modules:
  0.0 114.5 jit_solution(14110188978269305213)
XLA Ops:
  0.0 111.5 %shard_map.46 = bf16[1024,1024]{1,0:T(8,128)(2,1)} custom-call(bf16[1024,1024]{1,0:T(8,128)(2,1)} %tok_hbm.1, bf16[512,1280]{1,0:T(8,128)(2,1)} %w_hbm.1, bf16[512,1024]{1,0:T(8,128)(2,1)} %wo_hbm.1, s32[8,128]{1,0:T(8,128)} %bitcast.1), custom_call_target="tpu_custom_call" | custom-call | tf_op jit(solution)/shard_map/pallas_call | solution.py:384
  111.5 3.1 %copy.6 = bf16[1024,1024]{1,0:T(8,128)(2,1)} copy(bf16[1024,1024]{1,0:T(8,128)(2,1)} %shard_map.46) | data formatting | bytes 4194304

commit v5 on v4

--- a/solution.py
+++ b/solution.py
@@ -145,11 +145,12 @@
         kv = project(pl.ds(*CHUNKS[c]), kv_cols).astype(jnp.bfloat16)
         keys, values = keys_of(r, c)
         keys[...] = kv[:, :HEAD_DIM]
-        k_in.append([send(keys, keys, peer[XP])])
         values[...] = jnp.transpose(kv[:, HEAD_DIM:])
-        k_in[c].append(send(values, values, peer[XP]))
-        kv_core[c].append(send(keys, keys, peer[CORE]))
-        kv_core[c].append(send(values, values, peer[CORE]))
+
+    def send_kv(c):
+        refs = keys_of(r, c)
+        k_in.append([send(ref, ref, peer[XP]) for ref in refs])
+        kv_core[c].extend(send(ref, ref, peer[CORE]) for ref in refs)
 
     def forward_kv(c):
         for ref, cp in zip(keys_of(row_of[XP], c), k_in[c]):
@@ -269,27 +270,57 @@
         ctx_copy(i + 1).start()
         return state
 
-    def project_out(b):
-        rows = pl.ds(pl.multiple_of(b * QB, QB), QB)
-
-        def wait_piece(h, carry):
-            ctx_copy(b * HEADS + h).wait_recv()
-            return carry
-
-        lax.fori_loop(0, HEADS, wait_piece, 0)
+    def wait_pieces(first, end):
+        def wait_piece(i, carry):
+            ctx_copy(i).wait_recv()
+            return carry
+
+        lax.fori_loop(first, end, wait_piece, 0)
+
+    def heads(ref, b, first, end):
+        return jnp.concatenate([ref[b * HEADS + h] for h in range(first, end)], axis=1)
+
+    def out_rows(half_index, first, end):
+        size = (end - first) * HEAD_DIM
+        return pl.ds(pl.multiple_of(half_index * HID + first * HEAD_DIM, HEAD_DIM), size)
+
+    def out_copy(b, n):
+        at = (pl.ds(pl.multiple_of(b * QB, QB), QB), pl.ds(pl.multiple_of(n * 256, 256), 256))
+        return pltpu.make_async_copy(out_buf.at[at], out_hbm.at[at], out_sem.at[b * 4 + n])
+
+    def store_out(b, n, o):
+        out_buf[pl.ds(pl.multiple_of(b * QB, QB), QB), pl.ds(pl.multiple_of(n * 256, 256), 256)] = o.astype(jnp.bfloat16)
+        out_copy(b, n).start()
+
+    def out_product(b, n, end):
+        cols = pl.ds(pl.multiple_of(n * 256, 256), 256)
+        own = jnp.dot(heads(ctx_own, b, 0, HEADS), wo_buf[own_half, cols], preferred_element_type=jnp.float32)
+        rows = out_rows(1 - y, 0, end)
+        return own + jnp.dot(heads(ctx_peer, b, 0, end), wo_buf[rows, cols], preferred_element_type=jnp.float32)
+
+    def project_out(b, carry):
+        wait_pieces(b * HEADS, (b + 1) * HEADS)
 
         def out_tile(n, carry):
-            cols = pl.ds(pl.multiple_of(n * 256, 256), 256)
-            own, other = (jnp.concatenate([ref[b * HEADS + h] for h in range(HEADS)], axis=1) for ref in (ctx_own, ctx_peer))
-            o = jnp.dot(own, wo_buf[own_half, cols], preferred_element_type=jnp.float32) + jnp.dot(
-                other, wo_buf[peer_half, cols], preferred_element_type=jnp.float32
-            )
-            out_buf[rows, cols] = o.astype(jnp.bfloat16)
-            return carry
-
-        lax.fori_loop(0, HID // 256, out_tile, 0)
-        out = pltpu.make_async_copy(out_buf.at[rows], out_hbm.at[rows], out_sem.at[b])
-        out.start()
+            store_out(b, n, out_product(b, n, HEADS))
+            return carry
+
+        return lax.fori_loop(0, 4, out_tile, carry)
+
+    def project_last():
+        b, most = N_BLOCK - 1, HEADS - 2
+        wait_pieces(b * HEADS, b * HEADS + most)
+
+        def first_part(n, carry):
+            p_buf[2, pl.ds(pl.multiple_of(n * QB, QB), QB), :] = out_product(b, n, most)
+            return carry
+
+        lax.fori_loop(0, 4, first_part, 0)
+        wait_pieces(b * HEADS + most, TILES)
+        for n in range(4):
+            cols, rows = pl.ds(n * 256, 256), out_rows(1 - y, most, HEADS)
+            o = jnp.dot(heads(ctx_peer, b, most, HEADS), wo_buf[rows, cols], preferred_element_type=jnp.float32)
+            store_out(b, n, p_buf[2, pl.ds(n * QB, QB), :] + o)
 
     project_kv(0)
     forward_wq(0)
@@ -297,26 +328,31 @@
     project_kv(1)
     forward_wq(2)
     forward_wq(3)
+    send_kv(0)
+    send_kv(1)
     for cp in wq_f:
         cp.wait_recv()
     project_q(0)
     project_q(1)
+    project_kv(2)
+    send_kv(2)
     forward_kv(0)
     forward_kv(1)
-    project_kv(2)
     project_q(2)
     for c in (0, 1):
         wait_kv(c)
     prefetch(0, 1)
+    project_kv(3)
+    send_kv(3)
+    project_kv(4)
+    send_kv(4)
+    wo_x = [send_wo(0), send_wo(1)]
     forward_kv(2)
-    project_kv(3)
     wait_kv(2)
     prefetch(2)
     forward_kv(3)
-    project_kv(4)
-    wo_x = [send_wo(0), send_wo(1)]
+    forward_kv(4)
     project_q(3)
-    forward_kv(4)
     for c in (3, 4):
         wait_kv(c)
 
@@ -328,8 +364,10 @@
         else:
             state = tile(i, i, state, i + 1, 0, empty, every)
         if i % 2:
-            ctx_copy(i - 1).start()
-            ctx_copy(i).start()
+            for n in range(max(i - 1, 1), i + 1):
+                ctx_copy(n).start()
+        elif i == 0:
+            ctx_copy(0).start()
 
     pairs = HEADS // 2
     state = lax.fori_loop(pairs, 2 * pairs, two_tiles, state)
@@ -353,18 +391,14 @@
     for cp in wo_f:
         cp.wait_recv()
 
-    def last_block(b, carry):
-        project_out(b)
+    lax.fori_loop(0, N_BLOCK - 1, project_out, 0)
+    project_last()
+
+    def wait_out(i, carry):
+        out_copy(i // 4, i % 4).wait()
         return carry
 
-    lax.fori_loop(0, N_BLOCK, last_block, 0)
-
-    def wait_out(b, carry):
-        rows = pl.ds(pl.multiple_of(b * QB, QB), QB)
-        pltpu.make_async_copy(out_buf.at[rows], out_hbm.at[rows], out_sem.at[b]).wait()
-        return carry
-
-    lax.fori_loop(0, N_BLOCK, wait_out, 0)
+    lax.fori_loop(0, N_BLOCK * 4, wait_out, 0)
     for cp in sent:
         cp.wait_send()
 
@@ -408,7 +442,7 @@
                 dma((N_SEM,)),
                 dma((TILES,)),
                 dma((TILES,)),
-                dma((N_BLOCK,)),
+                dma((N_BLOCK * 4,)),
             ],
             compiler_params=pltpu.CompilerParams(
                 collective_id=0, has_side_effects=True, vmem_limit_bytes=67043328

time: 115 us -> 112 us (0.974)
  Pallas kernels: 111 us -> 109 us
    pallas_call x1, Pallas kernels: 111 us -> 109 us  [local_block(): pl.pallas_call(kernel, out_shape=jax.ShapeDtypeStruct(tokens.shape, bf16)...]
where the time goes in v5:
time: 112 us
  Pallas kernels  109 us (97%)
  local copies, waits for them, and re-layouts  3.08 us (3%)
    pallas_call x1, Pallas kernels, local_block(): pl.pallas_call(kernel, out_shape=jax.ShapeDtypeStruct(tokens.shape, bf16)...  109 us
    unnamed x1, local copies, waits for them, and re-layouts  3.08 us

profile of v5, /device:TPU:0, one launch (start us, length us, event | category | flops | bytes accessed | tf_op | source)
XLA Modules:
  0.0 111.9 jit_solution(12089745345124312862)
XLA Ops:
  0.0 108.8 %shard_map.46 = bf16[1024,1024]{1,0:T(8,128)(2,1)} custom-call(bf16[1024,1024]{1,0:T(8,128)(2,1)} %tok_hbm.1, bf16[512,1280]{1,0:T(8,128)(2,1)} %w_hbm.1, bf16[512,1024]{1,0:T(8,128)(2,1)} %wo_hbm.1, s32[8,128]{1,0:T(8,128)} %bitcast.1), custom_call_target="tpu_custom_call" | custom-call | tf_op jit(solution)/shard_map/pallas_call | solution.py:418
  108.8 3.1 %copy.6 = bf16[1024,1024]{1,0:T(8,128)(2,1)} copy(bf16[1024,1024]{1,0:T(8,128)(2,1)} %shard_map.46) | data formatting | bytes 4194304

commit v6 on v5

--- a/solution.py
+++ b/solution.py
@@ -37,16 +37,15 @@
 
 
 def kernel(
-    tok_hbm, w_hbm, wo_hbm, doc_hbm, out_hbm,
+    tok_hbm, w_hbm, wo_hbm, doc_hbm, out_ref,
     tok_own, tok_peer, w_buf, wo_buf, doc_buf, q_buf, qx_buf, k_buf, kx_buf, vw_buf, vn_buf, p_buf, top_buf, state_buf,
-    ctx_own, ctx_peer, loc_sem, send_sem, recv_sem, ctx_send, ctx_recv, out_sem,
+    ctx_own, ctx_peer, loc_sem, send_sem, recv_sem, ctx_send, ctx_recv,
 ):
     d, y, r = lax.axis_index("data"), lax.axis_index("col"), lax.axis_index("row")
     x, core = r // 2, r % 2
     row_of = {CORE: x * 2 + (1 - core), XP: (1 - x) * 2 + core, DIAG: (1 - x) * 2 + (1 - core)}
     y_peer = (d, 1 - y, r)
     peer = {k: (d, y, v) for k, v in row_of.items()}
-    out_buf = tok_own
 
     barrier = pltpu.get_barrier_semaphore()
     for p in (y_peer, peer[CORE], peer[XP], peer[DIAG]):
@@ -284,13 +283,8 @@
         size = (end - first) * HEAD_DIM
         return pl.ds(pl.multiple_of(half_index * HID + first * HEAD_DIM, HEAD_DIM), size)
 
-    def out_copy(b, n):
-        at = (pl.ds(pl.multiple_of(b * QB, QB), QB), pl.ds(pl.multiple_of(n * 256, 256), 256))
-        return pltpu.make_async_copy(out_buf.at[at], out_hbm.at[at], out_sem.at[b * 4 + n])
-
     def store_out(b, n, o):
-        out_buf[pl.ds(pl.multiple_of(b * QB, QB), QB), pl.ds(pl.multiple_of(n * 256, 256), 256)] = o.astype(jnp.bfloat16)
-        out_copy(b, n).start()
+        out_ref[pl.ds(pl.multiple_of(b * QB, QB), QB), pl.ds(pl.multiple_of(n * 256, 256), 256)] = o.astype(jnp.bfloat16)
 
     def out_product(b, n, end):
         cols = pl.ds(pl.multiple_of(n * 256, 256), 256)
@@ -344,30 +338,31 @@
     prefetch(0, 1)
     project_kv(3)
     send_kv(3)
+    forward_kv(2)
     project_kv(4)
     send_kv(4)
     wo_x = [send_wo(0), send_wo(1)]
-    forward_kv(2)
     wait_kv(2)
     prefetch(2)
     forward_kv(3)
     forward_kv(4)
-    project_q(3)
     for c in (3, 4):
         wait_kv(c)
 
     last = N_STEP - 1
     state = score_step(0, 0, last, load_state(0))
     for i in range(SLOTS):
-        if i + 1 < SLOTS:
+        if i == 0:
+            tile(0, 0, state)
+            ctx_copy(0).start()
+            state = score_step(1, 1, last, load_state(1))
+        elif i + 1 < SLOTS:
             state = tile(i, i, state, i + 1, i + 1, load_state(i + 1), (last,))
         else:
             state = tile(i, i, state, i + 1, 0, empty, every)
         if i % 2:
             for n in range(max(i - 1, 1), i + 1):
                 ctx_copy(n).start()
-        elif i == 0:
-            ctx_copy(0).start()
 
     pairs = HEADS // 2
     state = lax.fori_loop(pairs, 2 * pairs, two_tiles, state)
@@ -378,6 +373,7 @@
         wo_f.append(forward(wo_buf, shard(row_of[XP], p, half)))
 
     forward_wo(0)
+    project_q(3)
     state = lax.fori_loop(2 * pairs, 3 * pairs, two_tiles, state)
     forward_wo(1)
     state = lax.fori_loop(3 * pairs, 4 * pairs - 1, two_tiles, state)
@@ -394,11 +390,6 @@
     lax.fori_loop(0, N_BLOCK - 1, project_out, 0)
     project_last()
 
-    def wait_out(i, carry):
-        out_copy(i // 4, i % 4).wait()
-        return carry
-
-    lax.fori_loop(0, N_BLOCK * 4, wait_out, 0)
     for cp in sent:
         cp.wait_send()
 
@@ -417,9 +408,9 @@
         any_spec = pl.BlockSpec(memory_space=pl.ANY)
         return pl.pallas_call(
             kernel,
-            out_shape=jax.ShapeDtypeStruct(tokens.shape, bf16),
+            out_shape=pltpu.VMEM(tokens.shape, bf16),
             in_specs=[any_spec] * 4,
-            out_specs=any_spec,
+            out_specs=pl.BlockSpec(memory_space=pltpu.VMEM),
             scratch_shapes=[
                 pltpu.VMEM((ROWS, HID), bf16),
                 pltpu.VMEM((ROWS, HID), bf16),
@@ -442,10 +433,9 @@
                 dma((N_SEM,)),
                 dma((TILES,)),
                 dma((TILES,)),
-                dma((N_BLOCK * 4,)),
             ],
             compiler_params=pltpu.CompilerParams(
-                collective_id=0, has_side_effects=True, vmem_limit_bytes=67043328
+                collective_id=0, has_side_effects=True, vmem_limit_bytes=59 * 1024 * 1024
             ),
         )(tokens, w_qkv, w_out, doc_ids.reshape(8, 128))
 

time: 112 us -> 109 us (0.973)
  Pallas kernels: 109 us -> 107 us
  local copies, waits for them, and re-layouts: 3.08 us -> 1.32 us
    unnamed x1, local copies, waits for them, and re-layouts: 3.08 us -> 1.32 us
    pallas_call x1, Pallas kernels: 109 us -> 107 us  [local_block(): pl.pallas_call(kernel, out_shape=pltpu.VMEM(tokens.shape, bf16), in_specs...]
where the time goes in v6:
time: 109 us; the launch traced here: 108 us
  Pallas kernels  107 us (98%)
  local copies, waits for them, and re-layouts  1.32 us (1%)
    pallas_call x1, Pallas kernels, local_block(): pl.pallas_call(kernel, out_shape=pltpu.VMEM(tokens.shape, bf16), in_specs...  107 us

profile of v6, /device:TPU:0, one launch (start us, length us, event | category | flops | bytes accessed | tf_op | source)
XLA Modules:
  0.0 108.4 jit_solution(6961719167750835951)
XLA Ops:
  0.0 107.1 %shard_map.46 = bf16[1024,1024]{1,0:T(8,128)(2,1)S(1)} custom-call(bf16[1024,1024]{1,0:T(8,128)(2,1)} %tok_hbm.1, bf16[512,1280]{1,0:T(8,128)(2,1)} %w_hbm.1, bf16[512,1024]{1,0:T(8,128)(2,1)} %wo_hbm.1, s32[8,128]{1,0:T(8,128)} %bitcast.1), custom_call_target="tpu_custom_call" | custom-call | tf_op jit(solution)/shard_map/pallas_call | solution.py:409
  107.1 1.3 %copy.6 = bf16[1024,1024]{1,0:T(8,128)(2,1)} copy(bf16[1024,1024]{1,0:T(8,128)(2,1)S(1)} %shard_map.46) | data formatting | bytes 4194304

commit v7 on v6

--- a/solution.py
+++ b/solution.py
@@ -22,13 +22,13 @@
 GROUP = 128
 N_GROUP = KC // GROUP
 N_STEP = SEQ // KC
-CHUNKS = ((0, 256), (256, 256), (512, 256), (768, 128), (896, 128))
+CHUNKS = ((0, 256), (256, 256), (512, 256), (768, 128), (896, 64), (960, 64))
 W_PIECES = 4
 W_ROWS = SHARD // W_PIECES
 N_BLOCK = ROWS // QB
 TILES = HEADS * N_BLOCK
 SLOTS = 8
-N_SEM = 64
+N_SEM = 72
 CORE, XP, DIAG = 0, 1, 2
 EXP_SCALE = math.log2(math.e) / math.sqrt(HEAD_DIM)
 NT = (((1,), (1,)), ((), ()))
@@ -38,7 +38,7 @@
 
 def kernel(
     tok_hbm, w_hbm, wo_hbm, doc_hbm, out_ref,
-    tok_own, tok_peer, w_buf, wo_buf, doc_buf, q_buf, qx_buf, k_buf, kx_buf, vw_buf, vn_buf, p_buf, top_buf, state_buf,
+    tok_own, tok_peer, w_buf, wo_buf, doc_buf, q_buf, qx_buf, k_buf, kx_buf, vw_buf, vn_buf, vr_buf, vl_buf, p_buf, top_buf, state_buf,
     ctx_own, ctx_peer, loc_sem, send_sem, recv_sem, ctx_send, ctx_recv,
 ):
     d, y, r = lax.axis_index("data"), lax.axis_index("col"), lax.axis_index("row")
@@ -103,8 +103,10 @@
         def line_mask(i, carry):
             part, line, first = place(i)
             ids = as_column(doc_buf[part, pl.ds(line, 1), :])
-            hit = jnp.where(lane < 3, 1 - ids, jnp.where(lane < 6, ids, 0))
-            kx_buf[pl.ds(pl.multiple_of(first, 128), 128), :] = hit.astype(jnp.float32).astype(jnp.bfloat16)
+            hit = jnp.where(lane < 3, 1 - ids, jnp.where(lane < 6, ids, 0)).astype(jnp.float32).astype(jnp.bfloat16)
+            for n, at in enumerate(first):
+                size = 128 // len(first)
+                kx_buf[pl.ds(pl.multiple_of(at, size), size), :] = hit[n * size : (n + 1) * size]
             return carry
 
         return line_mask
@@ -115,10 +117,10 @@
         qx_buf[pl.ds(pl.multiple_of(i * 128, 128), 128), :] = jnp.where(hit == 1, -BF16_MAX, 0.0).astype(jnp.bfloat16)
         return carry
 
-    wide = key_mask(lambda i: (i // 6, i % 6, (i % 6) // 2 * 1024 + i // 6 * 256 + i % 2 * 128))
+    wide = key_mask(lambda i: (i // 6, i % 6, [(i % 6) // 2 * 1024 + i // 6 * 256 + i % 2 * 128]))
     lax.fori_loop(0, 24, wide, 0)
-    narrow = key_mask(lambda i: (i // 2, 6 + i % 2, 3072 + i % 2 * 512 + i // 2 * 128))
-    lax.fori_loop(0, 8, narrow, 0)
+    lax.fori_loop(0, 4, key_mask(lambda i: (i, 6, [3072 + i * 128])), 0)
+    lax.fori_loop(0, 4, key_mask(lambda i: (i, 7, [3584 + i * 64, 3840 + i * 64])), 0)
     lax.fori_loop(0, ROWS // 128, query_mask, 0)
 
     own_half = pl.ds(pl.multiple_of(y * HID, HID), HID)
@@ -136,7 +138,10 @@
 
     def keys_of(row, c):
         first, size = CHUNKS[c]
-        values = vw_buf.at[c * 4 + row] if size == 256 else vn_buf.at[(c - N_STEP + 1) * 4 + row]
+        if size == 64:
+            values = vr_buf.at[c - 4, pl.ds(pl.multiple_of(row * size, size), size)]
+        else:
+            values = vw_buf.at[c * 4 + row] if size == 256 else vn_buf.at[row]
         return k_buf.at[pl.ds(pl.multiple_of(first * 4 + row * size, size), size)], values
 
     def project_kv(c):
@@ -144,10 +149,13 @@
         kv = project(pl.ds(*CHUNKS[c]), kv_cols).astype(jnp.bfloat16)
         keys, values = keys_of(r, c)
         keys[...] = kv[:, :HEAD_DIM]
-        values[...] = jnp.transpose(kv[:, HEAD_DIM:])
+        values[...] = kv[:, HEAD_DIM:] if c >= 4 else jnp.transpose(kv[:, HEAD_DIM:])
 
     def send_kv(c):
         refs = keys_of(r, c)
+        if c >= 4:
+            kv_core[c] += [send(ref, ref, peer[k]) for k in (XP, DIAG, CORE) for ref in refs]
+            return
         k_in.append([send(ref, ref, peer[XP]) for ref in refs])
         kv_core[c].extend(send(ref, ref, peer[CORE]) for ref in refs)
 
@@ -220,7 +228,7 @@
         keys = pl.ds(j * KC, KC)
         factor = [to_keys(jnp.exp2(top_buf[slot, j * N_GROUP + g] - lse)) for g in range(N_GROUP)]
         weights = p_buf[slot, keys, :] * jnp.concatenate(factor, axis=0)
-        parts = [vw_buf[j * 4 + i] for i in range(4)] if j + 1 < N_STEP else [vn_buf[i] for i in range(8)]
+        parts = [vw_buf[j * 4 + i] for i in range(4)] if j + 1 < N_STEP else [*(vn_buf[i] for i in range(4)), vl_buf[0], vl_buf[1]]
         o = jnp.dot(jnp.concatenate(parts, axis=1), weights.astype(jnp.bfloat16), preferred_element_type=jnp.float32)
         return o if acc is None else acc + o
 
@@ -341,13 +349,16 @@
     forward_kv(2)
     project_kv(4)
     send_kv(4)
+    project_kv(5)
+    send_kv(5)
     wo_x = [send_wo(0), send_wo(1)]
     wait_kv(2)
+    forward_kv(3)
     prefetch(2)
-    forward_kv(3)
-    forward_kv(4)
-    for c in (3, 4):
+    for c in (3, 4, 5):
         wait_kv(c)
+        if c >= 4:
+            vl_buf[c - 4] = jnp.transpose(vr_buf[c - 4])
 
     last = N_STEP - 1
     state = score_step(0, 0, last, load_state(0))
@@ -422,7 +433,9 @@
                 pltpu.VMEM((SEQ, HEAD_DIM), bf16),
                 pltpu.VMEM((SEQ, HEAD_DIM), bf16),
                 pltpu.VMEM((12, HEAD_DIM, 256), bf16),
-                pltpu.VMEM((8, HEAD_DIM, 128), bf16),
+                pltpu.VMEM((4, HEAD_DIM, 128), bf16),
+                pltpu.VMEM((2, 256, HEAD_DIM), bf16),
+                pltpu.VMEM((2, HEAD_DIM, 256), bf16),
                 pltpu.VMEM((SLOTS, SEQ, QB), f32),
                 pltpu.VMEM((SLOTS, SEQ // GROUP, 8, QB), f32),
                 pltpu.VMEM((SLOTS, 2, 8, QB), f32),
@@ -435,7 +448,7 @@
                 dma((TILES,)),
             ],
             compiler_params=pltpu.CompilerParams(
-                collective_id=0, has_side_effects=True, vmem_limit_bytes=59 * 1024 * 1024
+                collective_id=0, has_side_effects=True, vmem_limit_bytes=61 * 1024 * 1024
             ),
         )(tokens, w_qkv, w_out, doc_ids.reshape(8, 128))
 

time: 109 us -> 109 us (level)
  no operation moved by 1% of the time
where the time goes in v7:
time: 109 us
  Pallas kernels  108 us (99%)
  local copies, waits for them, and re-layouts  1.32 us (1%)
    pallas_call x1, Pallas kernels, local_block(): pl.pallas_call(kernel, out_shape=pltpu.VMEM(tokens.shape, bf16), in_specs...  108 us

profile of v7, /device:TPU:0, one launch (start us, length us, event | category | flops | bytes accessed | tf_op | source)
XLA Modules:
  0.0 109.1 jit_solution(8846315384276487754)
XLA Ops:
  0.0 107.8 %shard_map.46 = bf16[1024,1024]{1,0:T(8,128)(2,1)S(1)} custom-call(bf16[1024,1024]{1,0:T(8,128)(2,1)} %tok_hbm.1, bf16[512,1280]{1,0:T(8,128)(2,1)} %w_hbm.1, bf16[512,1024]{1,0:T(8,128)(2,1)} %wo_hbm.1, s32[8,128]{1,0:T(8,128)} %bitcast.1), custom_call_target="tpu_custom_call" | custom-call | tf_op jit(solution)/shard_map/pallas_call | solution.py:420
  107.8 1.3 %copy.6 = bf16[1024,1024]{1,0:T(8,128)(2,1)} copy(bf16[1024,1024]{1,0:T(8,128)(2,1)S(1)} %shard_map.46) | data formatting | bytes 4194304

commit v8 on v7

--- a/solution.py
+++ b/solution.py
@@ -324,37 +324,36 @@
             o = jnp.dot(heads(ctx_peer, b, most, HEADS), wo_buf[rows, cols], preferred_element_type=jnp.float32)
             store_out(b, n, p_buf[2, pl.ds(n * QB, QB), :] + o)
 
-    project_kv(0)
+    def new_kv(c):
+        project_kv(c)
+        send_kv(c)
+
+    new_kv(0)
     forward_wq(0)
     forward_wq(1)
-    project_kv(1)
+    new_kv(1)
     forward_wq(2)
+    forward_kv(0)
     forward_wq(3)
-    send_kv(0)
-    send_kv(1)
+    forward_kv(1)
+    new_kv(2)
     for cp in wq_f:
         cp.wait_recv()
     project_q(0)
-    project_q(1)
-    project_kv(2)
-    send_kv(2)
-    forward_kv(0)
-    forward_kv(1)
-    project_q(2)
     for c in (0, 1):
         wait_kv(c)
     prefetch(0, 1)
-    project_kv(3)
-    send_kv(3)
+    new_kv(3)
     forward_kv(2)
-    project_kv(4)
-    send_kv(4)
-    project_kv(5)
-    send_kv(5)
+    project_q(1)
+    wait_kv(2)
+    prefetch(2)
+    new_kv(4)
+    new_kv(5)
     wo_x = [send_wo(0), send_wo(1)]
-    wait_kv(2)
     forward_kv(3)
-    prefetch(2)
+    project_q(2)
+    project_q(3)
     for c in (3, 4, 5):
         wait_kv(c)
         if c >= 4:
@@ -384,7 +383,6 @@
         wo_f.append(forward(wo_buf, shard(row_of[XP], p, half)))
 
     forward_wo(0)
-    project_q(3)
     state = lax.fori_loop(2 * pairs, 3 * pairs, two_tiles, state)
     forward_wo(1)
     state = lax.fori_loop(3 * pairs, 4 * pairs - 1, two_tiles, state)

time: 109 us -> 112 us (1.028)
  Pallas kernels: 108 us -> 111 us
    pallas_call x1, Pallas kernels: 108 us -> 111 us  [local_block(): pl.pallas_call(kernel, out_shape=pltpu.VMEM(tokens.shape, bf16), in_specs...]
where the time goes in v8:
time: 112 us
  Pallas kernels  111 us (99%)
  local copies, waits for them, and re-layouts  1.32 us (1%)
    pallas_call x1, Pallas kernels, local_block(): pl.pallas_call(kernel, out_shape=pltpu.VMEM(tokens.shape, bf16), in_specs...  111 us

profile of v8, /device:TPU:0, one launch (start us, length us, event | category | flops | bytes accessed | tf_op | source)
XLA Modules:
  0.0 112.2 jit_solution(16621292937871674346)
XLA Ops:
  0.0 110.8 %shard_map.46 = bf16[1024,1024]{1,0:T(8,128)(2,1)S(1)} custom-call(bf16[1024,1024]{1,0:T(8,128)(2,1)} %tok_hbm.1, bf16[512,1280]{1,0:T(8,128)(2,1)} %w_hbm.1, bf16[512,1024]{1,0:T(8,128)(2,1)} %wo_hbm.1, s32[8,128]{1,0:T(8,128)} %bitcast.1), custom_call_target="tpu_custom_call" | custom-call | tf_op jit(solution)/shard_map/pallas_call | solution.py:418
  110.8 1.3 %copy.6 = bf16[1024,1024]{1,0:T(8,128)(2,1)} copy(bf16[1024,1024]{1,0:T(8,128)(2,1)S(1)} %shard_map.46) | data formatting | bytes 4194304

commit v9 on v8

--- a/solution.py
+++ b/solution.py
@@ -23,8 +23,7 @@
 N_GROUP = KC // GROUP
 N_STEP = SEQ // KC
 CHUNKS = ((0, 256), (256, 256), (512, 256), (768, 128), (896, 64), (960, 64))
-W_PIECES = 4
-W_ROWS = SHARD // W_PIECES
+HALF_COLS = HID // 2
 N_BLOCK = ROWS // QB
 TILES = HEADS * N_BLOCK
 SLOTS = 8
@@ -72,7 +71,13 @@
     def shard(row, piece=0, size=SHARD):
         return pl.ds(pl.multiple_of(row * SHARD + piece * size, size), size)
 
-    kv_cols, q_cols = pl.ds(HID, 2 * HEAD_DIM), pl.ds(0, HID)
+    kv_cols, half = pl.ds(HID, 2 * HEAD_DIM), SHARD // 2
+
+    def send_wq(cols):
+        at = pl.ds(cols * HALF_COLS, HALF_COLS)
+        return [
+            send(w_hbm.at[pl.ds(p * half, half), at], w_buf.at[shard(r, p, half), at], peer[XP]) for p in (0, 1)
+        ]
 
     tok_in = []
     for first, size in CHUNKS:
@@ -80,10 +85,7 @@
         tok_in.append(send(tok_hbm.at[rows], tok_peer.at[rows], y_peer))
     wkv_x = send(w_hbm.at[:, kv_cols], w_buf.at[shard(r), kv_cols], peer[XP])
     doc_in = [send(doc_hbm, doc_buf.at[r], peer[k]) for k in (CORE, XP, DIAG)]
-    wq_x = [
-        send(w_hbm.at[pl.ds(p * W_ROWS, W_ROWS), q_cols], w_buf.at[shard(r, p, W_ROWS), q_cols], peer[XP])
-        for p in range(W_PIECES)
-    ]
+    wq_x = [send_wq(0)]
     w_core = send(w_hbm, w_buf.at[shard(r)], peer[CORE])
     wo_core = send(wo_hbm, wo_buf.at[shard(r)], peer[CORE])
     doc_local = local(doc_hbm, doc_buf.at[r], 0)
@@ -168,7 +170,7 @@
         for cp in kv_core[c]:
             cp.wait_recv()
 
-    def project_q(c):
+    def project_q(c, first=0, end=4):
         rows = pl.ds(c * QB, QB)
 
         def q_tile(n, carry):
@@ -176,7 +178,7 @@
             q_buf[rows, cols] = project(rows, cols).astype(jnp.bfloat16)
             return carry
 
-        lax.fori_loop(0, HID // 256, q_tile, 0)
+        lax.fori_loop(first, end, q_tile, 0)
 
     wkv_x.wait_recv()
     wkv_f = forward(w_buf, shard(row_of[XP]), kv_cols)
@@ -184,22 +186,28 @@
     tok_local.wait()
     w_core.wait_recv()
     wkv_f.wait_recv()
-    wq_f = []
-
-    def forward_wq(p):
-        wq_x[p].wait_recv()
-        wq_f.append(forward(w_buf, shard(row_of[XP], p, W_ROWS), q_cols))
-
-    half = SHARD // 2
+    wq_f = [[], []]
+
+    def forward_wq(cols, p):
+        wq_x[cols][p].wait_recv()
+        wq_f[cols].append(forward(w_buf, shard(row_of[XP], p, half), pl.ds(cols * HALF_COLS, HALF_COLS)))
+
+    def wait_wq(cols):
+        for cp in wq_f[cols]:
+            cp.wait_recv()
 
     def send_wo(p):
         return send(wo_hbm.at[pl.ds(p * half, half)], wo_buf.at[shard(r, p, half)], peer[XP])
 
     def tile_of(i):
+        block, head = i // 16 * 2 + i // 4 % 2, i // 8 % 2 * 4 + i % 4
         return (
-            pl.ds(pl.multiple_of((i // HEADS) * QB, QB), QB),
-            pl.ds(pl.multiple_of((i % HEADS) * HEAD_DIM, HEAD_DIM), HEAD_DIM),
+            pl.ds(pl.multiple_of(block * QB, QB), QB),
+            pl.ds(pl.multiple_of(head * HEAD_DIM, HEAD_DIM), HEAD_DIM),
         )
+
+    def tile_at(block, head):
+        return block // 2 * 16 + head // 4 * 8 + block % 2 * 4 + head % 4
 
     def over_keys(f, a):
         return f(a.reshape(a.shape[0] // 8, 8, QB), axis=0)
@@ -277,15 +285,15 @@
         ctx_copy(i + 1).start()
         return state
 
-    def wait_pieces(first, end):
-        def wait_piece(i, carry):
-            ctx_copy(i).wait_recv()
+    def wait_pieces(b, first, end):
+        def wait_piece(h, carry):
+            ctx_copy(tile_at(b, h)).wait_recv()
             return carry
 
         lax.fori_loop(first, end, wait_piece, 0)
 
     def heads(ref, b, first, end):
-        return jnp.concatenate([ref[b * HEADS + h] for h in range(first, end)], axis=1)
+        return jnp.concatenate([ref[tile_at(b, h)] for h in range(first, end)], axis=1)
 
     def out_rows(half_index, first, end):
         size = (end - first) * HEAD_DIM
@@ -301,7 +309,7 @@
         return own + jnp.dot(heads(ctx_peer, b, 0, end), wo_buf[rows, cols], preferred_element_type=jnp.float32)
 
     def project_out(b, carry):
-        wait_pieces(b * HEADS, (b + 1) * HEADS)
+        wait_pieces(b, 0, HEADS)
 
         def out_tile(n, carry):
             store_out(b, n, out_product(b, n, HEADS))
@@ -311,14 +319,14 @@
 
     def project_last():
         b, most = N_BLOCK - 1, HEADS - 2
-        wait_pieces(b * HEADS, b * HEADS + most)
+        wait_pieces(b, 0, most)
 
         def first_part(n, carry):
             p_buf[2, pl.ds(pl.multiple_of(n * QB, QB), QB), :] = out_product(b, n, most)
             return carry
 
         lax.fori_loop(0, 4, first_part, 0)
-        wait_pieces(b * HEADS + most, TILES)
+        wait_pieces(b, most, HEADS)
         for n in range(4):
             cols, rows = pl.ds(n * 256, 256), out_rows(1 - y, most, HEADS)
             o = jnp.dot(heads(ctx_peer, b, most, HEADS), wo_buf[rows, cols], preferred_element_type=jnp.float32)
@@ -329,30 +337,34 @@
         send_kv(c)
 
     new_kv(0)
-    forward_wq(0)
-    forward_wq(1)
+    forward_wq(0, 0)
+    forward_wq(0, 1)
+    forward_kv(0)
+    wait_wq(0)
+    project_q(0, 0, 2)
     new_kv(1)
-    forward_wq(2)
-    forward_kv(0)
-    forward_wq(3)
+    wq_x.append(send_wq(1))
+    project_q(1, 0, 2)
+    wait_kv(0)
+    prefetch(0)
     forward_kv(1)
+    wait_kv(1)
+    prefetch(1)
+    forward_wq(1, 0)
     new_kv(2)
-    for cp in wq_f:
-        cp.wait_recv()
-    project_q(0)
-    for c in (0, 1):
-        wait_kv(c)
-    prefetch(0, 1)
-    new_kv(3)
+    forward_wq(1, 1)
+    wait_wq(1)
+    project_q(0, 2, 4)
+    project_q(1, 2, 4)
     forward_kv(2)
-    project_q(1)
     wait_kv(2)
     prefetch(2)
+    new_kv(3)
+    project_q(2)
     new_kv(4)
     new_kv(5)
     wo_x = [send_wo(0), send_wo(1)]
     forward_kv(3)
-    project_q(2)
     project_q(3)
     for c in (3, 4, 5):
         wait_kv(c)

time: 112 us -> 113 us (level)
  no operation moved by 1% of the time
where the time goes in v9:
time: 113 us
  Pallas kernels  112 us (99%)
  local copies, waits for them, and re-layouts  1.32 us (1%)
    pallas_call x1, Pallas kernels, local_block(): pl.pallas_call(kernel, out_shape=pltpu.VMEM(tokens.shape, bf16), in_specs...  112 us

profile of v9, /device:TPU:0, one launch (start us, length us, event | category | flops | bytes accessed | tf_op | source)
XLA Modules:
  0.0 113.1 jit_solution(12898108480467729438)
XLA Ops:
  0.0 111.8 %shard_map.46 = bf16[1024,1024]{1,0:T(8,128)(2,1)S(1)} custom-call(bf16[1024,1024]{1,0:T(8,128)(2,1)} %tok_hbm.1, bf16[512,1280]{1,0:T(8,128)(2,1)} %w_hbm.1, bf16[512,1024]{1,0:T(8,128)(2,1)} %wo_hbm.1, s32[8,128]{1,0:T(8,128)} %bitcast.1), custom_call_target="tpu_custom_call" | custom-call | tf_op jit(solution)/shard_map/pallas_call | solution.py:430
  111.8 1.3 %copy.6 = bf16[1024,1024]{1,0:T(8,128)(2,1)} copy(bf16[1024,1024]{1,0:T(8,128)(2,1)S(1)} %shard_map.46) | data formatting | bytes 4194304

commit v10 on v9

--- a/solution.py
+++ b/solution.py
@@ -80,12 +80,16 @@
         ]
 
     tok_in = []
-    for first, size in CHUNKS:
-        rows = pl.ds(first, size)
-        tok_in.append(send(tok_hbm.at[rows], tok_peer.at[rows], y_peer))
+
+    def send_tokens(source, *chunks):
+        for c in chunks:
+            rows = pl.ds(*CHUNKS[c])
+            tok_in.append(send(source.at[rows], tok_peer.at[rows], y_peer))
+
+    send_tokens(tok_hbm, 0, 1)
     wkv_x = send(w_hbm.at[:, kv_cols], w_buf.at[shard(r), kv_cols], peer[XP])
     doc_in = [send(doc_hbm, doc_buf.at[r], peer[k]) for k in (CORE, XP, DIAG)]
-    wq_x = [send_wq(0)]
+    wq_x = []
     w_core = send(w_hbm, w_buf.at[shard(r)], peer[CORE])
     wo_core = send(wo_hbm, wo_buf.at[shard(r)], peer[CORE])
     doc_local = local(doc_hbm, doc_buf.at[r], 0)
@@ -136,7 +140,7 @@
     def forward(ref, *index):
         return send(ref.at[index], ref.at[index], peer[CORE])
 
-    k_in, kv_core = [], [[] for _ in CHUNKS]
+    k_in, kv_core = {}, [[] for _ in CHUNKS]
 
     def keys_of(row, c):
         first, size = CHUNKS[c]
@@ -158,7 +162,7 @@
         if c >= 4:
             kv_core[c] += [send(ref, ref, peer[k]) for k in (XP, DIAG, CORE) for ref in refs]
             return
-        k_in.append([send(ref, ref, peer[XP]) for ref in refs])
+        k_in[c] = [send(ref, ref, peer[XP]) for ref in refs]
         kv_core[c].extend(send(ref, ref, peer[CORE]) for ref in refs)
 
     def forward_kv(c):
@@ -180,6 +184,15 @@
 
         lax.fori_loop(first, end, q_tile, 0)
 
+    left = []
+
+    def gone(*copies):
+        for cp in copies:
+            cp.wait_send()
+            left.append(id(cp))
+
+    gone(wkv_x)
+    wq_x.append(send_wq(0))
     wkv_x.wait_recv()
     wkv_f = forward(w_buf, shard(row_of[XP]), kv_cols)
     w_local.wait()
@@ -336,40 +349,45 @@
         project_kv(c)
         send_kv(c)
 
-    new_kv(0)
     forward_wq(0, 0)
     forward_wq(0, 1)
+    gone(*wq_x[0])
+    wq_x.append(send_wq(1))
+    wait_wq(0)
+    gone(tok_in[0], tok_in[1])
+    send_tokens(tok_own, 2)
+    new_kv(0)
+    new_kv(1)
+    project_q(0, 0, 2)
+    project_q(1, 0, 2)
     forward_kv(0)
-    wait_wq(0)
-    project_q(0, 0, 2)
-    new_kv(1)
-    wq_x.append(send_wq(1))
-    project_q(1, 0, 2)
+    forward_kv(1)
+    forward_wq(1, 0)
+    forward_wq(1, 1)
     wait_kv(0)
     prefetch(0)
-    forward_kv(1)
+    gone(tok_in[2])
+    send_tokens(tok_own, 3, 4, 5)
     wait_kv(1)
     prefetch(1)
-    forward_wq(1, 0)
     new_kv(2)
-    forward_wq(1, 1)
     wait_wq(1)
     project_q(0, 2, 4)
     project_q(1, 2, 4)
     forward_kv(2)
     wait_kv(2)
     prefetch(2)
-    new_kv(3)
     project_q(2)
     new_kv(4)
     new_kv(5)
-    wo_x = [send_wo(0), send_wo(1)]
+    new_kv(3)
+    project_q(3)
     forward_kv(3)
-    project_q(3)
-    for c in (3, 4, 5):
+    for c in (4, 5, 3):
         wait_kv(c)
         if c >= 4:
             vl_buf[c - 4] = jnp.transpose(vr_buf[c - 4])
+    wo_x = [send_wo(0)]
 
     last = N_STEP - 1
     state = score_step(0, 0, last, load_state(0))
@@ -394,6 +412,8 @@
         wo_x[p].wait_recv()
         wo_f.append(forward(wo_buf, shard(row_of[XP], p, half)))
 
+    gone(wo_x[0])
+    wo_x.append(send_wo(1))
     forward_wo(0)
     state = lax.fori_loop(2 * pairs, 3 * pairs, two_tiles, state)
     forward_wo(1)
@@ -412,7 +432,8 @@
     project_last()
 
     for cp in sent:
-        cp.wait_send()
+        if id(cp) not in left:
+            cp.wait_send()
 
     def wait_sent(i, carry):
         ctx_copy(i).wait_send()

time: 113 us -> 127 us (1.12)
  Pallas kernels: 112 us -> 126 us
    pallas_call x1, Pallas kernels: 112 us -> 126 us  [local_block(): pl.pallas_call(kernel, out_shape=pltpu.VMEM(tokens.shape, bf16), in_specs...]
where the time goes in v10:
time: 127 us
  Pallas kernels  126 us (99%)
  local copies, waits for them, and re-layouts  1.32 us (1%)
    pallas_call x1, Pallas kernels, local_block(): pl.pallas_call(kernel, out_shape=pltpu.VMEM(tokens.shape, bf16), in_specs...  126 us

profile of v10, /device:TPU:0, one launch (start us, length us, event | category | flops | bytes accessed | tf_op | source)
XLA Modules:
  0.0 127.2 jit_solution(17358850037249003988)
XLA Ops:
  0.0 125.9 %shard_map.46 = bf16[1024,1024]{1,0:T(8,128)(2,1)S(1)} custom-call(bf16[1024,1024]{1,0:T(8,128)(2,1)} %tok_hbm.1, bf16[512,1280]{1,0:T(8,128)(2,1)} %w_hbm.1, bf16[512,1024]{1,0:T(8,128)(2,1)} %wo_hbm.1, s32[8,128]{1,0:T(8,128)} %bitcast.1), custom_call_target="tpu_custom_call" | custom-call | tf_op jit(solution)/shard_map/pallas_call | solution.py:451
  125.9 1.3 %copy.6 = bf16[1024,1024]{1,0:T(8,128)(2,1)} copy(bf16[1024,1024]{1,0:T(8,128)(2,1)S(1)} %shard_map.46) | data formatting | bytes 4194304

commit v11 on v6

--- a/solution.py
+++ b/solution.py
@@ -327,12 +327,10 @@
     for cp in wq_f:
         cp.wait_recv()
     project_q(0)
-    project_q(1)
     project_kv(2)
     send_kv(2)
     forward_kv(0)
     forward_kv(1)
-    project_q(2)
     for c in (0, 1):
         wait_kv(c)
     prefetch(0, 1)
@@ -352,6 +350,8 @@
     last = N_STEP - 1
     state = score_step(0, 0, last, load_state(0))
     for i in range(SLOTS):
+        if i == 4:
+            project_q(1)
         if i == 0:
             tile(0, 0, state)
             ctx_copy(0).start()
@@ -364,6 +364,7 @@
             for n in range(max(i - 1, 1), i + 1):
                 ctx_copy(n).start()
 
+    project_q(2)
     pairs = HEADS // 2
     state = lax.fori_loop(pairs, 2 * pairs, two_tiles, state)
     wo_f = []

time: 109 us -> 113 us (1.037)
  Pallas kernels: 107 us -> 111 us
    pallas_call x1, Pallas kernels: 107 us -> 111 us  [local_block(): pl.pallas_call(kernel, out_shape=pltpu.VMEM(tokens.shape, bf16), in_specs...]
where the time goes in v11:
time: 113 us
  Pallas kernels  111 us (98%)
  local copies, waits for them, and re-layouts  1.32 us (1%)
    pallas_call x1, Pallas kernels, local_block(): pl.pallas_call(kernel, out_shape=pltpu.VMEM(tokens.shape, bf16), in_specs...  111 us

profile of v11, /device:TPU:0, one launch (start us, length us, event | category | flops | bytes accessed | tf_op | source)
XLA Modules:
  0.0 112.5 jit_solution(17282982362633012973)
XLA Ops:
  0.0 111.2 %shard_map.46 = bf16[1024,1024]{1,0:T(8,128)(2,1)S(1)} custom-call(bf16[1024,1024]{1,0:T(8,128)(2,1)} %tok_hbm.1, bf16[512,1280]{1,0:T(8,128)(2,1)} %w_hbm.1, bf16[512,1024]{1,0:T(8,128)(2,1)} %wo_hbm.1, s32[8,128]{1,0:T(8,128)} %bitcast.1), custom_call_target="tpu_custom_call" | custom-call | tf_op jit(solution)/shard_map/pallas_call | solution.py:410
  111.2 1.3 %copy.6 = bf16[1024,1024]{1,0:T(8,128)(2,1)} copy(bf16[1024,1024]{1,0:T(8,128)(2,1)S(1)} %shard_map.46) | data formatting | bytes 4194304

commit v12 on v6

--- a/solution.py
+++ b/solution.py
@@ -346,6 +346,7 @@
     prefetch(2)
     forward_kv(3)
     forward_kv(4)
+    project_q(3)
     for c in (3, 4):
         wait_kv(c)
 
@@ -373,7 +374,6 @@
         wo_f.append(forward(wo_buf, shard(row_of[XP], p, half)))
 
     forward_wo(0)
-    project_q(3)
     state = lax.fori_loop(2 * pairs, 3 * pairs, two_tiles, state)
     forward_wo(1)
     state = lax.fori_loop(3 * pairs, 4 * pairs - 1, two_tiles, state)

time: 109 us -> 108 us (level)
  no operation moved by 1% of the time
where the time goes in v12:
time: 108 us
  Pallas kernels  107 us (99%)
  local copies, waits for them, and re-layouts  1.32 us (1%)
    pallas_call x1, Pallas kernels, local_block(): pl.pallas_call(kernel, out_shape=pltpu.VMEM(tokens.shape, bf16), in_specs...  107 us

profile of v12, /device:TPU:0, one launch (start us, length us, event | category | flops | bytes accessed | tf_op | source)
XLA Modules:
  0.0 108.3 jit_solution(17993778381330764898)
XLA Ops:
  0.0 107.0 %shard_map.46 = bf16[1024,1024]{1,0:T(8,128)(2,1)S(1)} custom-call(bf16[1024,1024]{1,0:T(8,128)(2,1)} %tok_hbm.1, bf16[512,1280]{1,0:T(8,128)(2,1)} %w_hbm.1, bf16[512,1024]{1,0:T(8,128)(2,1)} %wo_hbm.1, s32[8,128]{1,0:T(8,128)} %bitcast.1), custom_call_target="tpu_custom_call" | custom-call | tf_op jit(solution)/shard_map/pallas_call | solution.py:409
  107.0 1.3 %copy.6 = bf16[1024,1024]{1,0:T(8,128)(2,1)} copy(bf16[1024,1024]{1,0:T(8,128)(2,1)S(1)} %shard_map.46) | data formatting | bytes 4194304
